TPU v7x, 32 devices: a whole 2x2x4 slice. The times are simulated.
32 devices in a mesh: freq: 8 (over z, y), pts: 4 (over x, core).
Axes of the slice: x: 2, y: 2, z: 4, core: 2. Of those that a mesh axis runs over, the one named last changes fastest.
Arguments:
- direct: bfloat16 [8, 512, 6144], P('freq', None, 'pts'), may hold values from -6 to 6
- onsets: int32 [8, 6144], P('freq', 'pts'), may hold values from 64 to 511
- left_bases: bfloat16 [128, 24, 24, 2, 8, 256], P('freq', 'pts'), may hold values from -0.4375 to 0.4375
- right_bases: bfloat16 [128, 24, 24, 2, 8, 256], P('freq', 'pts'), may hold values from -0.25 to 0.25
- tile_ranks: int32 [128, 24, 24], P('freq', 'pts'), may hold values from 1 to 8
Outputs:
- plus_field: float32 [8, 512, 6144], P('freq', None, 'pts')
- minus_field: float32 [8, 512, 6144], P('freq', None, 'pts')
All inputs are finite; a program needn't handle non-finite values.
Results may differ from a plain program's by a relative error of at most 0.017.
Values may be sent and summed in bfloat16 or wider, within the bound.
A program may use at most 256 MiB of HBM per device.

v0:
```python
import math

import jax
import jax.numpy as jnp
from jax import lax
from jax.sharding import PartitionSpec as P

NB = 256
K = 8
F = 128
ITERS = 3
NT = 512


def band_tables(freq_total, sample_total):
    bins = lax.broadcasted_iota(jnp.int32, (freq_total, sample_total), 0) + 1
    moments = lax.broadcasted_iota(jnp.int32, (freq_total, sample_total), 1)
    phases = 2.0 * math.pi / sample_total * (bins * moments % sample_total).astype(jnp.float32)
    scaling = 1.0 / math.sqrt(sample_total)
    cosine = jnp.cos(phases) * scaling
    sine = jnp.sin(phases) * scaling
    return (jnp.stack([cosine, -sine]), jnp.stack([2.0 * cosine, -2.0 * sine]))


def contract(spec, left_part, right_part):
    return jnp.einsum(spec, left_part, right_part, preferred_element_type=jnp.float32)


def body(direct, onsets, left_bases, right_bases, tile_ranks):
    forward_exact, inverse_exact = band_tables(F, NT)
    forward_table = forward_exact.astype(jnp.bfloat16)
    inverse_table = inverse_exact.astype(jnp.bfloat16)
    point_here = direct.shape[0]
    cells_here = direct.shape[2]
    tile_here = cells_here // NB
    freq_here = left_bases.shape[0]
    tile_count = left_bases.shape[2]
    point_total = point_here * lax.axis_size("freq")
    group_count = lax.axis_size("pts")
    moments = lax.broadcasted_iota(jnp.int32, direct.shape, 1)
    window = (moments < onsets[:, None, :]).astype(jnp.float32)
    rank_index = lax.broadcasted_iota(jnp.int32, tile_ranks.shape + (K,), 3)
    rank_mask = (rank_index < tile_ranks[..., None]).astype(jnp.bfloat16)[..., None]

    def to_band(history):
        samples = history.astype(jnp.bfloat16)
        spectrum = jnp.einsum(
            "cft,ptn->fcpn", forward_table, samples, preferred_element_type=jnp.float32
        )
        spectrum = spectrum.astype(jnp.bfloat16).reshape(F, 2, point_here, cells_here)
        return lax.all_to_all(spectrum, "freq", split_axis=0, concat_axis=2, tiled=True)

    def to_time(spectrum):
        returned = lax.all_to_all(
            spectrum.astype(jnp.bfloat16), "freq", split_axis=2, concat_axis=0, tiled=True
        )
        return (
            jnp.einsum("cft,fcpn->ptn", inverse_table, returned, preferred_element_type=jnp.float32)
            * window
        )

    stacked_left = left_bases.reshape(freq_here, tile_here, tile_count, 2 * K, NB)
    stacked_right = right_bases.reshape(freq_here, tile_here, tile_count, 2 * K, NB)
    lines = 2 * point_total

    def tiled_lines(spectrum):
        tiled = spectrum.reshape(freq_here, lines, tile_here, NB)
        return tiled.transpose(0, 2, 1, 3)

    def conj_terms(product):
        parts = product.reshape(freq_here, tile_here, tile_count, 2, K, 2, point_total)
        real_part = parts[:, :, :, 0, :, 0] + parts[:, :, :, 1, :, 1]
        imag_part = parts[:, :, :, 0, :, 1] - parts[:, :, :, 1, :, 0]
        real_part = real_part.astype(jnp.bfloat16) * rank_mask
        imag_part = imag_part.astype(jnp.bfloat16) * rank_mask
        upper = jnp.concatenate([real_part, imag_part], axis=-1)
        lower = jnp.concatenate([-imag_part, real_part], axis=-1)
        return jnp.concatenate([upper, lower], axis=3)

    def forward_apply(spectrum):
        everywhere = lax.all_gather(tiled_lines(spectrum), "pts", axis=1, tiled=True)
        terms = conj_terms(contract("fijqb,fjnb->fijqn", stacked_right, everywhere))
        result = contract("fijqb,fijqn->finb", stacked_left, terms).astype(jnp.bfloat16)
        return result.transpose(0, 2, 1, 3).reshape(freq_here, 2, point_total, cells_here)

    def adjoint_apply(spectrum):
        terms = conj_terms(contract("fijqb,finb->fijqn", stacked_left, tiled_lines(spectrum)))
        partial_value = contract("fijqb,fijqn->fjnb", stacked_right, terms)
        partial_value = partial_value.astype(jnp.bfloat16)
        arrived = lax.all_to_all(
            partial_value.reshape(freq_here, group_count, tile_here, lines, NB),
            "pts",
            split_axis=1,
            concat_axis=1,
            tiled=True,
        )
        total = jnp.sum(arrived.astype(jnp.float32), axis=1).astype(jnp.bfloat16)
        return total.transpose(0, 2, 1, 3).reshape(freq_here, 2, point_total, cells_here)

    history = direct.astype(jnp.float32)
    plus_field = history
    minus_field = jnp.zeros_like(history)
    for iteration in range(ITERS):
        reflected = to_time(forward_apply(to_band(history)))
        minus_field = minus_field + reflected
        history = to_time(adjoint_apply(to_band(reflected)))
        plus_field = plus_field + history
    return (plus_field, minus_field)


def solution(mesh):
    return jax.shard_map(
        body,
        mesh=mesh,
        in_specs=(
            P("freq", None, "pts"),
            P("freq", "pts"),
            P("freq", "pts", None, None, None, None),
            P("freq", "pts", None, None, None, None),
            P("freq", "pts", None),
        ),
        out_specs=(P("freq", None, "pts"), P("freq", None, "pts")),
        check_vma=False,
    )
```

profile of v0, /device:TPU:0, one launch (start us, length us, event | category | flops | bytes accessed | tf_op | source)
XLA Modules:
  0.0 982.5 jit_solution(17184750675674506579)
XLA Ops:
  11.5 27.3 %all_to_all.195 = bf16[128,2,1,1536]{3,1,2,0:T(2,128)(2,1)S(1)} all-to-all(bf16[128,2,1,1536]{3,1,2,0:T(2,128)(2,1)S(1)} %copy.109), channel_id=1, replica_groups=mesh['freq'=8,'pts'=4] {'freq'}, dimensions={0} | all-to-all | bytes 1572864 | tf_op jit(solution)/shard_map/all_to_all | solution.py:51
  41.2 27.6 %all-gather.4.cloned.1.call-done = bf16[16,24,16,256]{3,2,1,0:T(8,128)(2,1)} async-done(((bf16[16,6,16,256]{3,2,1,0:T(8,128)(2,1)}), bf16[16,24,16,256]{3,2,1,0:T(8,128)(2,1)}) %all-gather.4.cloned.1.call-update) | async-done | bytes 3145744 | tf_op jit(solution)/shard_map/all_gather | solution.py:81
  68.8 30.2 %convolution_bitcast_fusion.2 = f32[16,6,24,16,16]{3,4,1,2,0:T(8,128)} fusion(bf16[16,24,16,256]{3,2,1,0:T(8,128)(2,1)} %all-gather.4.cloned.1.call-done, bf16[16,6,24,2,8,256]{5,4,3,2,1,0:T(8,128)(2,1)} %param.8), kind=kOutput, calls=%fused_computation.2 | convolution fusion | flops 301989888 | bytes 24379392 | tf_op jit(solution)/shard_map/fijqb,fjnb->fijqn/dot_general | solution.py:26
  98.9 18.6 %copy.113 = f32[16,6,24,16,16]{2,4,3,1,0:T(8,128)} copy(f32[16,6,24,16,16]{3,4,1,2,0:T(8,128)} %convolution_bitcast_fusion.2) | data formatting | bytes 4718592 | tf_op jit(solution)/shard_map/fijqb,fjnb->fijqn/transpose | solution.py:26
  117.6 5.7 fusion.178
  123.3 14.9 %fusion.135 = bf16[16,16,6,256]{3,1,2,0:T(8,128)(2,1)S(1)} fusion(bf16[16,6,24,16,256]{4,3,2,1,0:T(8,128)(2,1)} %bitcast.577, bf16[16,6,24,8,8]{2,4,3,1,0:T(8,128)(2,1)S(1)} %get-tuple-element.25, bf16[16,6,24,8,8]{2,4,3,1,0:T(8,128)(2,1)S(1)} %get-tuple-element.18, bf16[16,6,24,8,8]{2,4,3,1,0:T(8,128)(2,1)S(1)} %get-tuple-element.19), kind=kOutput, calls=%fused_computation.167 | convolution fusion | flops 307101696 | bytes 20545536 | tf_op jit(solution)/shard_map/fijqb,fijqn->finb/dot_general | solution.py:26
  140.8 5.5 all-to-all-start.1
  146.4 20.5 %all-to-all-done.1 = bf16[16,2,8,1536]{3,1,0,2:T(2,128)(2,1)S(1)} async-done(((bf16[16,2,8,1536]{3,1,0,2:T(2,128)(2,1)}), bf16[16,2,8,1536]{3,1,0,2:T(2,128)(2,1)S(1)}, u32[]{:S(2)}, u32[]{:S(2)}) %all-to-all-start.1) | async-done | bytes 786464 | tf_op jit(solution)/shard_map/all_to_all | solution.py:54
  170.7 24.1 %all_to_all.196 = bf16[128,2,1,1536]{3,1,2,0:T(2,128)(2,1)S(1)} all-to-all(bf16[128,2,1,1536]{3,1,2,0:T(2,128)(2,1)S(1)} %copy.124), channel_id=1, replica_groups=mesh['freq'=8,'pts'=4] {'freq'}, dimensions={0} | all-to-all | bytes 1572864 | tf_op jit(solution)/shard_map/all_to_all | solution.py:51
  195.7 22.2 %fusion.8 = f32[16,6,16,24,16]{3,2,4,1,0:T(8,128)} fusion(bf16[16,6,24,16,256]{4,3,2,1,0:T(8,128)(2,1)} %bitcast.578, bf16[16,16,6,256]{3,2,0,1:T(8,128)(2,1)S(1)} %reshape.397), kind=kOutput, calls=%fused_computation.11 | convolution fusion | flops 301989888 | bytes 22020096 | tf_op jit(solution)/shard_map/fijqb,finb->fijqn/dot_general | solution.py:26
  217.9 5.7 fusion.176
  223.6 4.1 maximum_maximum_fusion
  227.7 17.8 %copy.133 = bf16[16,6,24,16,16]{3,4,1,2,0:T(8,128)(2,1)} copy(bf16[16,6,24,16,16]{2,4,3,1,0:T(8,128)(2,1)} %maximum_maximum_fusion) | data formatting | bytes 2359296 | tf_op jit(solution)/shard_map/concatenate | solution.py:78
  245.5 15.9 %bitcast_convert_fusion.2 = bf16[16,24,16,256]{3,2,1,0:T(8,128)(2,1)S(1)} fusion(bf16[16,6,24,16,16]{3,4,1,2,0:T(8,128)(2,1)} %copy.133, bf16[16,6,24,2,8,256]{5,4,3,2,1,0:T(8,128)(2,1)} %param.8), kind=kOutput, calls=%fused_computation.50 | convolution fusion | flops 303562752 | bytes 23199744 | tf_op jit(solution)/shard_map/fijqb,fijqn->fjnb/dot_general | solution.py:26
  261.7 39.4 %all_to_all.197 = bf16[16,4,6,16,256]{4,3,2,0,1:T(8,128)(2,1)S(1)} all-to-all(bf16[16,4,6,16,256]{4,3,2,0,1:T(8,128)(2,1)S(1)} %copy.135), channel_id=1, replica_groups=mesh['freq'=8,'pts'=4] {'pts'}, dimensions={1} | all-to-all | bytes 6291456 | tf_op jit(solution)/shard_map/all_to_all | solution.py:90
  305.7 23.2 %all_to_all.198 = bf16[16,2,8,1536]{3,1,0,2:T(2,128)(2,1)S(1)} all-to-all(bf16[16,2,8,1536]{3,1,0,2:T(2,128)(2,1)S(1)} %copy.138), channel_id=1, replica_groups=mesh['freq'=8,'pts'=4] {'freq'}, dimensions={2} | all-to-all | bytes 1572864 | tf_op jit(solution)/shard_map/all_to_all | solution.py:54
  332.7 23.1 %all_to_all.199 = bf16[128,2,1,1536]{3,1,2,0:T(2,128)(2,1)S(1)} all-to-all(bf16[128,2,1,1536]{3,1,2,0:T(2,128)(2,1)S(1)} %copy.141), channel_id=1, replica_groups=mesh['freq'=8,'pts'=4] {'freq'}, dimensions={0} | all-to-all | bytes 1572864 | tf_op jit(solution)/shard_map/all_to_all | solution.py:51
  358.1 27.0 %all-gather.6.cloned.1.call-done = bf16[16,24,16,256]{3,2,1,0:T(8,128)(2,1)} async-done(((bf16[16,6,16,256]{3,2,1,0:T(8,128)(2,1)}), bf16[16,24,16,256]{3,2,1,0:T(8,128)(2,1)}) %all-gather.6.cloned.1.call-update) | async-done | bytes 3145744 | tf_op jit(solution)/shard_map/all_gather | solution.py:81
  385.1 30.4 %convolution_bitcast_fusion.1 = f32[16,6,24,16,16]{3,4,1,2,0:T(8,128)} fusion(bf16[16,24,16,256]{3,2,1,0:T(8,128)(2,1)} %all-gather.6.cloned.1.call-done, bf16[16,6,24,2,8,256]{5,4,3,2,1,0:T(8,128)(2,1)} %param.8), kind=kOutput, calls=%fused_computation.1 | convolution fusion | flops 301989888 | bytes 24379392 | tf_op jit(solution)/shard_map/fijqb,fjnb->fijqn/dot_general | solution.py:26
  415.5 18.6 %copy.146 = f32[16,6,24,16,16]{2,4,3,1,0:T(8,128)} copy(f32[16,6,24,16,16]{3,4,1,2,0:T(8,128)} %convolution_bitcast_fusion.1) | data formatting | bytes 4718592 | tf_op jit(solution)/shard_map/fijqb,fjnb->fijqn/transpose | solution.py:26
  434.1 5.7 fusion.174
  439.8 15.1 %fusion.140 = bf16[16,16,6,256]{3,1,2,0:T(8,128)(2,1)S(1)} fusion(bf16[16,6,24,16,256]{4,3,2,1,0:T(8,128)(2,1)} %bitcast.579, bf16[16,6,24,8,8]{2,4,3,1,0:T(8,128)(2,1)S(1)} %get-tuple-element.23, bf16[16,6,24,8,8]{2,4,3,1,0:T(8,128)(2,1)S(1)} %get-tuple-element.14, bf16[16,6,24,8,8]{2,4,3,1,0:T(8,128)(2,1)S(1)} %get-tuple-element.15), kind=kOutput, calls=%fused_computation.168 | convolution fusion | flops 307101696 | bytes 20545536 | tf_op jit(solution)/shard_map/fijqb,fijqn->finb/dot_general | solution.py:26
  456.7 25.8 %all_to_all.200 = bf16[16,2,8,1536]{3,1,0,2:T(2,128)(2,1)S(1)} all-to-all(bf16[16,2,8,1536]{3,1,0,2:T(2,128)(2,1)S(1)} %copy.153), channel_id=1, replica_groups=mesh['freq'=8,'pts'=4] {'freq'}, dimensions={2} | all-to-all | bytes 1572864 | tf_op jit(solution)/shard_map/all_to_all | solution.py:54
  486.3 23.7 %all_to_all.201 = bf16[128,2,1,1536]{3,1,2,0:T(2,128)(2,1)S(1)} all-to-all(bf16[128,2,1,1536]{3,1,2,0:T(2,128)(2,1)S(1)} %copy.156), channel_id=1, replica_groups=mesh['freq'=8,'pts'=4] {'freq'}, dimensions={0} | all-to-all | bytes 1572864 | tf_op jit(solution)/shard_map/all_to_all | solution.py:51
  510.9 22.2 %fusion.4 = f32[16,6,16,24,16]{3,2,4,1,0:T(8,128)} fusion(bf16[16,6,24,16,256]{4,3,2,1,0:T(8,128)(2,1)} %bitcast.580, bf16[16,16,6,256]{3,2,0,1:T(8,128)(2,1)S(1)} %reshape.399), kind=kOutput, calls=%fused_computation.7 | convolution fusion | flops 301989888 | bytes 22020096 | tf_op jit(solution)/shard_map/fijqb,finb->fijqn/dot_general | solution.py:26
  533.1 5.7 fusion.172
  538.8 4.1 maximum_maximum_fusion.1
  542.9 17.8 %copy.165 = bf16[16,6,24,16,16]{3,4,1,2,0:T(8,128)(2,1)} copy(bf16[16,6,24,16,16]{2,4,3,1,0:T(8,128)(2,1)} %maximum_maximum_fusion.1) | data formatting | bytes 2359296 | tf_op jit(solution)/shard_map/concatenate | solution.py:78
  560.7 15.9 %bitcast_convert_fusion.1 = bf16[16,24,16,256]{3,2,1,0:T(8,128)(2,1)S(1)} fusion(bf16[16,6,24,16,16]{3,4,1,2,0:T(8,128)(2,1)} %copy.165, bf16[16,6,24,2,8,256]{5,4,3,2,1,0:T(8,128)(2,1)} %param.8), kind=kOutput, calls=%fused_computation.49 | convolution fusion | flops 303562752 | bytes 23199744 | tf_op jit(solution)/shard_map/fijqb,fijqn->fjnb/dot_general | solution.py:26
  576.9 39.4 %all_to_all.202 = bf16[16,4,6,16,256]{4,3,2,0,1:T(8,128)(2,1)S(1)} all-to-all(bf16[16,4,6,16,256]{4,3,2,0,1:T(8,128)(2,1)S(1)} %copy.167), channel_id=1, replica_groups=mesh['freq'=8,'pts'=4] {'pts'}, dimensions={1} | all-to-all | bytes 6291456 | tf_op jit(solution)/shard_map/all_to_all | solution.py:90
  620.9 23.2 %all_to_all.203 = bf16[16,2,8,1536]{3,1,0,2:T(2,128)(2,1)S(1)} all-to-all(bf16[16,2,8,1536]{3,1,0,2:T(2,128)(2,1)S(1)} %copy.170), channel_id=1, replica_groups=mesh['freq'=8,'pts'=4] {'freq'}, dimensions={2} | all-to-all | bytes 1572864 | tf_op jit(solution)/shard_map/all_to_all | solution.py:54
  648.0 23.5 %all_to_all.204 = bf16[128,2,1,1536]{3,1,2,0:T(2,128)(2,1)S(1)} all-to-all(bf16[128,2,1,1536]{3,1,2,0:T(2,128)(2,1)S(1)} %copy.173), channel_id=1, replica_groups=mesh['freq'=8,'pts'=4] {'freq'}, dimensions={0} | all-to-all | bytes 1572864 | tf_op jit(solution)/shard_map/all_to_all | solution.py:51
  673.7 27.1 %all-gather.8.cloned.1.call-done = bf16[16,24,16,256]{3,2,1,0:T(8,128)(2,1)} async-done(((bf16[16,6,16,256]{3,2,1,0:T(8,128)(2,1)}), bf16[16,24,16,256]{3,2,1,0:T(8,128)(2,1)}) %all-gather.8.cloned.1.call-update) | async-done | bytes 3145744 | tf_op jit(solution)/shard_map/all_gather | solution.py:81
  700.8 30.2 %convolution_bitcast_fusion = f32[16,6,24,16,16]{3,4,1,2,0:T(8,128)} fusion(bf16[16,24,16,256]{3,2,1,0:T(8,128)(2,1)} %all-gather.8.cloned.1.call-done, bf16[16,6,24,2,8,256]{5,4,3,2,1,0:T(8,128)(2,1)} %param.8), kind=kOutput, calls=%fused_computation | convolution fusion | flops 301989888 | bytes 24379392 | tf_op jit(solution)/shard_map/fijqb,fjnb->fijqn/dot_general | solution.py:26
  731.0 18.6 %copy.178 = f32[16,6,24,16,16]{2,4,3,1,0:T(8,128)} copy(f32[16,6,24,16,16]{3,4,1,2,0:T(8,128)} %convolution_bitcast_fusion) | data formatting | bytes 4718592 | tf_op jit(solution)/shard_map/fijqb,fjnb->fijqn/transpose | solution.py:26
  749.6 5.7 fusion.170
  755.3 14.8 %fusion.145 = bf16[16,16,6,256]{3,1,2,0:T(8,128)(2,1)S(1)} fusion(bf16[16,6,24,16,256]{4,3,2,1,0:T(8,128)(2,1)} %bitcast.581, bf16[16,6,24,8,8]{2,4,3,1,0:T(8,128)(2,1)S(1)} %get-tuple-element.21, bf16[16,6,24,8,8]{2,4,3,1,0:T(8,128)(2,1)S(1)} %get-tuple-element.10, bf16[16,6,24,8,8]{2,4,3,1,0:T(8,128)(2,1)S(1)} %get-tuple-element.11), kind=kOutput, calls=%fused_computation.169 | convolution fusion | flops 307101696 | bytes 20545536 | tf_op jit(solution)/shard_map/fijqb,fijqn->finb/dot_general | solution.py:26
  776.2 25.8 %all_to_all.205 = bf16[16,2,8,1536]{3,1,0,2:T(2,128)(2,1)S(1)} all-to-all(bf16[16,2,8,1536]{3,1,0,2:T(2,128)(2,1)S(1)} %copy.185), channel_id=1, replica_groups=mesh['freq'=8,'pts'=4] {'freq'}, dimensions={2} | all-to-all | bytes 1572864 | tf_op jit(solution)/shard_map/all_to_all | solution.py:54
  805.9 23.7 %all_to_all.206 = bf16[128,2,1,1536]{3,1,2,0:T(2,128)(2,1)S(1)} all-to-all(bf16[128,2,1,1536]{3,1,2,0:T(2,128)(2,1)S(1)} %copy.188), channel_id=1, replica_groups=mesh['freq'=8,'pts'=4] {'freq'}, dimensions={0} | all-to-all | bytes 1572864 | tf_op jit(solution)/shard_map/all_to_all | solution.py:51
  830.6 22.2 %fusion = f32[16,6,16,24,16]{3,2,4,1,0:T(8,128)} fusion(bf16[16,6,24,16,256]{4,3,2,1,0:T(8,128)(2,1)} %bitcast.582, bf16[16,16,6,256]{3,2,0,1:T(8,128)(2,1)S(1)} %reshape.401), kind=kOutput, calls=%fused_computation.3 | convolution fusion | flops 301989888 | bytes 22020096 | tf_op jit(solution)/shard_map/fijqb,finb->fijqn/dot_general | solution.py:26
  852.8 5.7 fusion.168
  858.5 4.1 maximum_maximum_fusion.2
  862.5 17.8 %copy.197 = bf16[16,6,24,16,16]{3,4,1,2,0:T(8,128)(2,1)} copy(bf16[16,6,24,16,16]{2,4,3,1,0:T(8,128)(2,1)} %maximum_maximum_fusion.2) | data formatting | bytes 2359296 | tf_op jit(solution)/shard_map/concatenate | solution.py:78
  880.4 15.9 %bitcast_convert_fusion = bf16[16,24,16,256]{3,2,1,0:T(8,128)(2,1)S(1)} fusion(bf16[16,6,24,16,16]{3,4,1,2,0:T(8,128)(2,1)} %copy.197, bf16[16,6,24,2,8,256]{5,4,3,2,1,0:T(8,128)(2,1)} %param.8), kind=kOutput, calls=%fused_computation.48 | convolution fusion | flops 303562752 | bytes 23199744 | tf_op jit(solution)/shard_map/fijqb,fijqn->fjnb/dot_general | solution.py:26
  896.6 39.4 %all_to_all.207 = bf16[16,4,6,16,256]{4,3,2,0,1:T(8,128)(2,1)S(1)} all-to-all(bf16[16,4,6,16,256]{4,3,2,0,1:T(8,128)(2,1)S(1)} %copy.199), channel_id=1, replica_groups=mesh['freq'=8,'pts'=4] {'pts'}, dimensions={1} | all-to-all | bytes 6291456 | tf_op jit(solution)/shard_map/all_to_all | solution.py:90
  943.7 4.2 all-to-all-start.14
  952.9 15.2 %all-to-all-done.14 = bf16[16,2,8,1536]{3,1,0,2:T(2,128)(2,1)} async-done(((bf16[16,2,8,1536]{3,1,0,2:T(2,128)(2,1)}), bf16[16,2,8,1536]{3,1,0,2:T(2,128)(2,1)}, u32[]{:S(2)}, u32[]{:S(2)}) %all-to-all-start.14) | async-done | bytes 786464 | tf_op jit(solution)/shard_map/all_to_all | solution.py:54
  969.3 3.8 fusion.43
  (122 shorter events, 69.6 us)
Async XLA Ops:
  7.2 61.6 %all-gather.4.cloned.1.call-start = ((), (), s32[]{:S(2)}) async-start(), calls=%async_computation.15 | async-start | bytes 3932160 | tf_op jit(solution)/shard_map/all_gather | solution.py:81
  8.5 158.5 %copy-start.11 = (bf16[1,128,512]{2,1,0:T(8,128)(2,1)}, bf16[1,128,512]{2,1,0:T(8,128)(2,1)S(1)}, u32[]{:S(2)}) copy-start(bf16[1,128,512]{2,1,0:T(8,128)(2,1)S(1)} %get-tuple-element.26) | copy-start | bytes 393220
  8.5 158.5 %copy-start.16 = (bf16[1,128,512]{2,1,0:T(8,128)(2,1)}, bf16[1,128,512]{2,1,0:T(8,128)(2,1)S(1)}, u32[]{:S(2)}) copy-start(bf16[1,128,512]{2,1,0:T(8,128)(2,1)S(1)} %get-tuple-element.27) | copy-start | bytes 393220
  8.5 159.1 %copy-start.7 = (bf16[1,128,512]{2,1,0:T(8,128)(2,1)}, bf16[1,128,512]{2,1,0:T(8,128)(2,1)S(1)}, u32[]{:S(2)}) copy-start(bf16[1,128,512]{2,1,0:T(8,128)(2,1)S(1)} %get-tuple-element.29) | copy-start | bytes 393220
  38.7 2.4 copy-start.21
  138.1 8.2 copy-start.22
  140.8 26.1 %all-to-all-start.1 = ((bf16[16,2,8,1536]{3,1,0,2:T(2,128)(2,1)}), bf16[16,2,8,1536]{3,1,0,2:T(2,128)(2,1)S(1)}, u32[]{:S(2)}, u32[]{:S(2)}) async-start(bf16[16,2,8,1536]{3,1,0,2:T(2,128)(2,1)} %copy.121), calls=%async_computation.1 | async-start | bytes 1572864 | tf_op jit(solution)/shard_map/all_to_all | solution.py:54
  146.3 238.8 %all-gather.6.cloned.1.call-start = ((), (), s32[]{:S(2)}) async-start(), calls=%async_computation.16 | async-start | bytes 3932160 | tf_op jit(solution)/shard_map/all_gather | solution.py:81
  167.7 1.7 copy-start.2
  304.2 24.8 %copy-start.12 = (bf16[1,128,512]{2,1,0:T(8,128)(2,1)S(1)}, bf16[1,128,512]{2,1,0:T(8,128)(2,1)}, u32[]{:S(2)}) copy-start(bf16[1,128,512]{2,1,0:T(8,128)(2,1)} %copy-done.11) | copy-start | bytes 393220
  304.2 24.8 %copy-start.17 = (bf16[1,128,512]{2,1,0:T(8,128)(2,1)S(1)}, bf16[1,128,512]{2,1,0:T(8,128)(2,1)}, u32[]{:S(2)}) copy-start(bf16[1,128,512]{2,1,0:T(8,128)(2,1)} %copy-done.16) | copy-start | bytes 393220
  328.9 2.4 copy-start.8
  329.7 1.6 copy-start.1
  358.1 342.8 %all-gather.8.cloned.1.call-start = ((), (), s32[]{:S(2)}) async-start(), calls=%async_computation.17 | async-start | bytes 3932160 | tf_op jit(solution)/shard_map/all_gather | solution.py:81
  483.2 1.7 copy-start.5
  619.4 24.8 %copy-start.13 = (bf16[1,128,512]{2,1,0:T(8,128)(2,1)S(1)}, bf16[1,128,512]{2,1,0:T(8,128)(2,1)}, u32[]{:S(2)}) copy-start(bf16[1,128,512]{2,1,0:T(8,128)(2,1)} %copy-done.11) | copy-start | bytes 393220
  619.4 24.8 %copy-start.18 = (bf16[1,128,512]{2,1,0:T(8,128)(2,1)S(1)}, bf16[1,128,512]{2,1,0:T(8,128)(2,1)}, u32[]{:S(2)}) copy-start(bf16[1,128,512]{2,1,0:T(8,128)(2,1)} %copy-done.16) | copy-start | bytes 393220
  644.1 2.5 copy-start.9
  644.9 1.7 copy-start.4
  771.4 30.7 %copy-start.3 = (f32[1,512,1536]{1,2,0:T(8,128)S(1)}, f32[1,512,1536]{1,2,0:T(8,128)}, u32[]{:S(2)}) copy-start(f32[1,512,1536]{1,2,0:T(8,128)} %copy-done.2) | copy-start | bytes 9437188
  774.3 27.8 %copy-start.6 = (f32[1,512,1536]{1,2,0:T(8,128)S(1)}, f32[1,512,1536]{1,2,0:T(8,128)}, u32[]{:S(2)}) copy-start(f32[1,512,1536]{1,2,0:T(8,128)} %copy-done.5) | copy-start | bytes 9437188
  774.3 27.8 %copy-start.14 = (bf16[1,128,512]{2,1,0:T(8,128)(2,1)S(1)}, bf16[1,128,512]{2,1,0:T(8,128)(2,1)}, u32[]{:S(2)}) copy-start(bf16[1,128,512]{2,1,0:T(8,128)(2,1)} %copy-done.11) | copy-start | bytes 393220
  774.3 27.9 %copy-start.19 = (bf16[1,128,512]{2,1,0:T(8,128)(2,1)S(1)}, bf16[1,128,512]{2,1,0:T(8,128)(2,1)}, u32[]{:S(2)}) copy-start(bf16[1,128,512]{2,1,0:T(8,128)(2,1)} %copy-done.16) | copy-start | bytes 393220
  802.2 2.4 copy-start.10
  940.9 9.6 copy-start
  943.7 24.4 %all-to-all-start.14 = ((bf16[16,2,8,1536]{3,1,0,2:T(2,128)(2,1)}), bf16[16,2,8,1536]{3,1,0,2:T(2,128)(2,1)}, u32[]{:S(2)}, u32[]{:S(2)}) async-start(bf16[16,2,8,1536]{3,1,0,2:T(2,128)(2,1)} %copy.202), calls=%async_computation.14 | async-start | bytes 1572864 | tf_op jit(solution)/shard_map/all_to_all | solution.py:54
  950.5 18.8 %copy-start.15 = (bf16[1,128,512]{2,1,0:T(8,128)(2,1)S(1)}, bf16[1,128,512]{2,1,0:T(8,128)(2,1)}, u32[]{:S(2)}) copy-start(bf16[1,128,512]{2,1,0:T(8,128)(2,1)} %copy-done.11) | copy-start | bytes 393220
  950.5 18.8 %copy-start.20 = (bf16[1,128,512]{2,1,0:T(8,128)(2,1)S(1)}, bf16[1,128,512]{2,1,0:T(8,128)(2,1)}, u32[]{:S(2)}) copy-start(bf16[1,128,512]{2,1,0:T(8,128)(2,1)} %copy-done.16) | copy-start | bytes 393220
Sparse Core Ops, SparseCore 0:
  41.2 27.5 all-gather.3
  358.2 26.9 all-gather.5
  673.9 26.9 all-gather.7
where the time goes:
time: 993 us; the launch traced here: 982 us
  blocking collectives  362 us (36%)
  matrix products  264 us (27%)
  local copies, waits for them, and re-layouts  163 us (16%)
  waiting for transfers between devices  117 us (12%)
  other arithmetic  52.6 us (5%)
  between operations  14.9 us (2%)
    dot_general x12, matrix products, contract(): jnp.einsum(spec, left_part, right_part, preferred_element_type=jnp.float32)  250 us
    all_to_all x6, blocking collectives, to_band(): lax.all_to_all(spectrum, 'freq', split_axis=0, concat_axis=2, tiled=True)  145 us
    all_to_all x3, blocking collectives, adjoint_apply(): lax.all_to_all(partial_value.reshape(freq_here, group_count, tile_here, l...  118 us
    all_to_all x4, blocking collectives, to_time(): lax.all_to_all(spectrum.astype(jnp.bfloat16), 'freq', split_axis=2, conca...  98.1 us
    all_gather x3, waiting for transfers between devices, forward_apply(): lax.all_gather(tiled_lines(spectrum), 'pts', axis=1, tiled=True)  81.7 us
    transpose x3, local copies, waits for them, and re-layouts, contract(): jnp.einsum(spec, left_part, right_part, preferred_element_type=jnp.float32)  55.9 us
    concatenate x3, local copies, waits for them, and re-layouts, conj_terms(): return jnp.concatenate([upper, lower], axis=3)  53.5 us
    all_to_all x2, waiting for transfers between devices, to_time(): lax.all_to_all(spectrum.astype(jnp.bfloat16), 'freq', split_axis=2, conca...  35.7 us
  transfers between devices with their start and end apart: 5, of which 5 were waited for; matrix products, arithmetic and copies ran while one was open for 1% of the time, Pallas kernels for 0%

commit v1 on v0

v1 whole, which is shorter than its diff:
```python
import functools
import math

import jax
import jax.numpy as jnp
from jax import lax
from jax.experimental import pallas as pl
from jax.experimental.pallas import tpu as pltpu
from jax.sharding import PartitionSpec as P

NB = 256
K = 8
F = 128
ITERS = 3
NT = 512
CORES = 2
MESH = pl.DeviceIdType.MESH
f32 = jnp.float32
bf16 = jnp.bfloat16


def band_tables(freq_total, sample_total):
    bins = lax.broadcasted_iota(jnp.int32, (freq_total, sample_total), 0) + 1
    moments = lax.broadcasted_iota(jnp.int32, (freq_total, sample_total), 1)
    phases = 2.0 * math.pi / sample_total * (bins * moments % sample_total).astype(f32)
    scaling = 1.0 / math.sqrt(sample_total)
    cosine = jnp.cos(phases) * scaling
    sine = jnp.sin(phases) * scaling
    return (jnp.stack([cosine, -sine], 1), jnp.stack([2.0 * cosine, -2.0 * sine], 1))


def dot_nt(a, b):
    return lax.dot_general(a, b, (((1,), (1,)), ((), ())), preferred_element_type=f32)


def dot_nn(a, b):
    return lax.dot_general(a, b, (((1,), (0,)), ((), ())), preferred_element_type=f32)


def block_mask(group, lines):
    shape = (group * lines, group * 2 * K)
    row = lax.broadcasted_iota(jnp.int32, shape, 0) // lines
    column = lax.broadcasted_iota(jnp.int32, shape, 1) // (2 * K)
    return row == column


def coefficients(x, basis, mask):
    points, width = x.shape[0] // 2, basis.shape[0] * 2 * K
    product = dot_nt(x, basis.reshape(width, NB))
    lane = lax.broadcasted_iota(jnp.int32, (points, width), 1)
    first = (lane // K) % 2 == 0
    real, imag = product[:points], product[points:]

    def other(value):
        return jnp.where(first, pltpu.roll(value, width - K, 1), -pltpu.roll(value, K, 1))

    both = jnp.concatenate([real + other(imag), imag - other(real)], axis=0)
    return (both * mask).astype(bf16)


def expand(terms, mask, group):
    return jnp.where(mask, jnp.concatenate([terms] * group, axis=0), jnp.zeros((), bf16))


class Places:
    def __init__(self, freq_size, pts_size):
        self.freq_size, self.pts_size = freq_size, pts_size
        self.columns = pts_size // CORES
        self.freq = lax.axis_index("freq")
        self.pts = lax.axis_index("pts")
        self.core = self.pts % CORES
        self.column = self.pts // CORES

    def freq_peer(self, step):
        return lax.rem(self.freq + step, self.freq_size)

    def freq_source(self, step):
        return lax.rem(self.freq + self.freq_size - step, self.freq_size)

    def sibling(self):
        return self.column * CORES + 1 - self.core

    def column_peer(self, step):
        return lax.rem(self.column + step, self.columns)

    def greet(self):
        barrier = pltpu.get_barrier_semaphore()
        for step in range(1, self.freq_size):
            pl.semaphore_signal(barrier, 1, device_id={"freq": self.freq_peer(step)}, device_id_type=MESH)
        pl.semaphore_signal(barrier, 1, device_id={"pts": self.sibling()}, device_id_type=MESH)
        for step in range(1, self.columns):
            peer = self.column_peer(step) * CORES + self.core
            pl.semaphore_signal(barrier, 1, device_id={"pts": peer}, device_id_type=MESH)
        pl.semaphore_wait(barrier, self.freq_size - 1 + 1 + self.columns - 1)


def remote(src, dst, send, recv, **device):
    return pltpu.make_async_remote_copy(
        src_ref=src, dst_ref=dst, send_sem=send, recv_sem=recv, device_id=device, device_id_type=MESH
    )


def load_bases(left_hbm, right_hbm, left, right, sems):
    copies = []
    for f in range(left.shape[0]):
        copies.append(pltpu.make_async_copy(right_hbm.at[f], right.at[f], sems.at[0, f]))
        copies.append(pltpu.make_async_copy(left_hbm.at[f], left.at[f], sems.at[1, f]))
    return copies


def rows_of(index, rows):
    return pl.ds(pl.multiple_of(index * rows, rows), rows)


def tile_of(index):
    return pl.ds(pl.multiple_of(index * NB, NB), NB)


def forward_kernel(
    sizes, spectrum, left_hbm, right_hbm, mask, order, back, result,
    left, right, got, total, outgoing, basis_sem,
    to_send, to_recv, home_send, home_recv, sib_send, sib_recv, col_send, col_recv,
    relay_send, relay_recv, ret_send, ret_recv, ret_home,
):
    freq_size, pts_size, rows, lines = sizes
    at = Places(freq_size, pts_size)
    freq_here, tiles = left.shape[0], left.shape[1]
    loads = load_bases(left_hbm, right_hbm, left, right, basis_sem)
    for copy in loads:
        copy.start()
    at.greet()

    def to_copy(j, step):
        peer = at.freq_peer(step)
        return remote(
            spectrum.at[rows_of(peer, rows), tile_of(j)],
            got.at[at.pts, j, rows_of(at.freq, rows), :],
            to_send.at[j, step], to_recv.at[j, step], freq=peer,
        )

    def home_copy(j):
        return pltpu.make_async_copy(
            spectrum.at[rows_of(at.freq, rows), tile_of(j)],
            got.at[at.pts, j, rows_of(at.freq, rows), :],
            home_send.at[j],
        )

    def sib_copy(j):
        return remote(
            got.at[at.pts, j], got.at[at.pts, j], sib_send.at[j], sib_recv.at[j], pts=at.sibling()
        )

    def col_copy(j, step):
        return remote(
            got.at[at.pts, j], got.at[at.pts, j], col_send.at[j, step], col_recv.at[j, step],
            pts=at.column_peer(step) * CORES + at.core,
        )

    def relay_copy(j, step):
        owner = lax.rem(at.column + at.columns - step, at.columns) * CORES + at.core
        return remote(
            got.at[owner, j], got.at[owner, j], relay_send.at[j, step], relay_recv.at[j, step],
            pts=at.sibling(),
        )

    def send(j, carry):
        for step in range(1, freq_size):
            to_copy(j, step).start()
        home_copy(j).start()
        return carry

    lax.fori_loop(0, tiles, send, 0)
    total[...] = jnp.zeros_like(total)
    spread = block_mask(tiles, lines)
    for copy in loads:
        copy.wait()

    def compute(owner, j):
        column = owner * tiles + j
        ordered = dot_nn(order[...], got[owner, j]).astype(bf16)
        terms = [
            coefficients(ordered[f * lines : (f + 1) * lines], right[f, :, column], mask[column, f : f + 1])
            for f in range(freq_here)
        ]
        for f in range(freq_here):
            total[f] += dot_nn(
                expand(terms[f], spread, tiles), left[f, :, column].reshape(tiles * 2 * K, NB)
            )

    def advance(j, carry):
        @pl.when(j < tiles)
        def _():
            for step in range(1, freq_size):
                to_copy(j, step).wait_recv()
            home_copy(j).wait()
            for step in range(1, at.columns):
                col_copy(j, step).start()
            sib_copy(j).start()

        @pl.when(j >= 1)
        def _():
            for step in range(1, at.columns):
                col_copy(j - 1, step).wait_recv()
                relay_copy(j - 1, step).start()

        @pl.when(j < tiles)
        def _():
            compute(at.pts, j)
            sib_copy(j).wait_recv()
            compute(at.sibling(), j)

        @pl.when(j >= 1)
        def _():
            for step in range(1, at.columns):
                source = lax.rem(at.column + at.columns - step, at.columns)
                compute(source * CORES + at.core, j - 1)
                relay_copy(j - 1, step).wait_recv()
                compute(source * CORES + 1 - at.core, j - 1)

        return carry

    lax.fori_loop(0, tiles + 1, advance, 0)
    finish = returning(at, rows, outgoing, result, ret_send, ret_recv, ret_home)
    for j in range(tiles):
        value = total[:, j * lines : (j + 1) * lines, :].reshape(freq_here * lines, NB)
        outgoing[j] = dot_nn(back[...], value.astype(bf16)).astype(bf16)
        finish.start(j)

    def drain(j, carry):
        for step in range(1, freq_size):
            to_copy(j, step).wait_send()
        sib_copy(j).wait_send()
        for step in range(1, at.columns):
            col_copy(j, step).wait_send()
            relay_copy(j, step).wait_send()
        finish.wait(j)
        return carry

    lax.fori_loop(0, tiles, drain, 0)


class returning:
    def __init__(self, at, rows, outgoing, result, send, recv, home):
        self.at, self.rows = at, rows
        self.outgoing, self.result = outgoing, result
        self.send, self.recv, self.home = send, recv, home

    def copy(self, j, step):
        peer = self.at.freq_peer(step)
        return remote(
            self.outgoing.at[j, rows_of(peer, self.rows), :],
            self.result.at[rows_of(self.at.freq, self.rows), tile_of(j)],
            self.send.at[j, step], self.recv.at[j, step], freq=peer,
        )

    def own(self, j):
        return pltpu.make_async_copy(
            self.outgoing.at[j, rows_of(self.at.freq, self.rows), :],
            self.result.at[rows_of(self.at.freq, self.rows), tile_of(j)],
            self.home.at[j],
        )

    def start(self, j):
        for step in range(1, self.at.freq_size):
            self.copy(j, step).start()
        self.own(j).start()

    def wait(self, j):
        for step in range(1, self.at.freq_size):
            self.copy(j, step).wait()
        self.own(j).wait()


def adjoint_kernel(
    sizes, spectrum, left_hbm, right_hbm, mask, order, back, result,
    left, right, got, total, outgoing, pair_out, pair_in, col_out, col_in, basis_sem,
    to_send, to_recv, home_send, pair_send, pair_recv, col_send, col_recv,
    ret_send, ret_recv, ret_home,
):
    freq_size, pts_size, rows, lines = sizes
    at = Places(freq_size, pts_size)
    freq_here, tiles = left.shape[0], left.shape[1]
    loads = load_bases(left_hbm, right_hbm, left, right, basis_sem)
    for copy in loads:
        copy.start()
    at.greet()

    def to_copy(j, step):
        peer = at.freq_peer(step)
        return remote(
            spectrum.at[rows_of(peer, rows), tile_of(j)],
            got.at[j, rows_of(at.freq, rows), :],
            to_send.at[j, step], to_recv.at[j, step], freq=peer,
        )

    def home_copy(j):
        return pltpu.make_async_copy(
            spectrum.at[rows_of(at.freq, rows), tile_of(j)],
            got.at[j, rows_of(at.freq, rows), :],
            home_send.at[j],
        )

    def send(j, carry):
        for step in range(1, freq_size):
            to_copy(j, step).start()
        home_copy(j).start()
        return carry

    lax.fori_loop(0, tiles, send, 0)
    total[...] = jnp.zeros_like(total)
    spread = block_mask(tiles, lines)
    for copy in loads:
        copy.wait()

    def advance(j, carry):
        for step in range(1, freq_size):
            to_copy(j, step).wait_recv()
        home_copy(j).wait()
        ordered = dot_nn(order[...], got[j]).astype(bf16)

        def group(owner, carry):
            span = pl.ds(owner * tiles, tiles)
            terms = [
                coefficients(ordered[f * lines : (f + 1) * lines], left[f, j, span], mask[j, owner, f : f + 1])
                for f in range(freq_here)
            ]
            for f in range(freq_here):
                total[owner, f] += dot_nn(
                    expand(terms[f], spread, tiles), right[f, j, span].reshape(tiles * 2 * K, NB)
                )
            return carry

        lax.fori_loop(0, pts_size, group, 0)
        return carry

    lax.fori_loop(0, tiles, advance, 0)

    def part(owner, j):
        piece = total[owner, :, pl.ds(pl.multiple_of(j * lines, lines), lines), :]
        return piece.reshape(freq_here * lines, NB)

    def pair_copy(j, step):
        return remote(
            pair_out.at[step, j], pair_in.at[step, j], pair_send.at[step, j], pair_recv.at[step, j],
            pts=at.sibling(),
        )

    def col_copy(j, step):
        return remote(
            col_out.at[step, j], col_in.at[step, j], col_send.at[step, j], col_recv.at[step, j],
            pts=at.column_peer(step) * CORES + at.core,
        )

    finish = returning(at, rows, outgoing, result, ret_send, ret_recv, ret_home)
    for step in list(range(1, at.columns)) + [0]:

        def pair_start(j, carry, step=step):
            owner = at.column_peer(step) * CORES + 1 - at.core
            pair_out[step, j] = part(owner, j).astype(bf16)
            pair_copy(j, step).start()
            return carry

        lax.fori_loop(0, tiles, pair_start, 0)
    for step in range(1, at.columns):

        def col_start(j, carry, step=step):
            pair_copy(j, step).wait_recv()
            owner = at.column_peer(step) * CORES + at.core
            col_out[step, j] = (part(owner, j) + pair_in[step, j].astype(f32)).astype(bf16)
            col_copy(j, step).start()
            return carry

        lax.fori_loop(0, tiles, col_start, 0)

    def close(j, carry):
        pair_copy(j, 0).wait_recv()
        value = part(at.pts, j) + pair_in[0, j].astype(f32)
        for step in range(1, at.columns):
            col_copy(j, step).wait_recv()
            value = value + col_in[step, j].astype(f32)
        outgoing[j] = dot_nn(back[...], value.astype(bf16)).astype(bf16)
        finish.start(j)
        return carry

    lax.fori_loop(0, tiles, close, 0)

    def drain(j, carry):
        for step in range(1, freq_size):
            to_copy(j, step).wait_send()
        for step in range(at.columns):
            pair_copy(j, step).wait_send()
        for step in range(1, at.columns):
            col_copy(j, step).wait_send()
        finish.wait(j)
        return carry

    lax.fori_loop(0, tiles, drain, 0)


def exchange_call(kind, sizes, spectrum, left, right, mask, order, back):
    freq_size, pts_size, rows, lines = sizes
    freq_here, tiles, tile_count = left.shape[:3]
    block = freq_size * rows
    columns = pts_size // CORES
    dma = pltpu.SemaphoreType.DMA
    bases = [pltpu.VMEM(left.shape, bf16), pltpu.VMEM(right.shape, bf16)]
    outgoing = pltpu.VMEM((tiles, block, NB), bf16)
    to_sems = [dma((tiles, freq_size)), dma((tiles, freq_size)), dma((tiles,))]
    ret_sems = [dma((tiles, freq_size)), dma((tiles, freq_size)), dma((tiles,))]
    if kind == "forward":
        kernel = forward_kernel
        scratch = bases + [
            pltpu.VMEM((pts_size, tiles, block, NB), bf16),
            pltpu.VMEM((freq_here, tiles * lines, NB), f32),
            outgoing,
            dma((2, freq_here)),
        ] + to_sems[:2] + [dma((tiles,)), dma((tiles,))] + [dma((tiles,)), dma((tiles,))] + [
            dma((tiles, columns)) for _ in range(4)
        ] + ret_sems
    else:
        kernel = adjoint_kernel
        pairs = [pltpu.VMEM((columns, tiles, block, NB), bf16) for _ in range(4)]
        scratch = bases + [
            pltpu.VMEM((tiles, block, NB), bf16),
            pltpu.VMEM((pts_size, freq_here, tiles * lines, NB), f32),
            outgoing,
        ] + pairs + [dma((2, freq_here))] + to_sems + [dma((columns, tiles)) for _ in range(4)] + ret_sems
    vmem = pl.BlockSpec(memory_space=pltpu.VMEM)
    hbm = pl.BlockSpec(memory_space=pl.ANY)
    return pl.pallas_call(
        functools.partial(kernel, sizes),
        out_shape=jax.ShapeDtypeStruct(spectrum.shape, bf16),
        name=kind,
        in_specs=[vmem, hbm, hbm, vmem, vmem, vmem],
        out_specs=vmem,
        scratch_shapes=scratch,
        compiler_params=pltpu.CompilerParams(
            collective_id=1 if kind == "forward" else 2,
            has_side_effects=True,
            vmem_limit_bytes=60 * 2**20,
        ),
    )(spectrum, left, right, mask, order, back)


def body(freq_size, pts_size, direct, onsets, left_bases, right_bases, tile_ranks):
    forward_exact, inverse_exact = band_tables(F, NT)
    forward_table = forward_exact.astype(bf16).reshape(2 * F, NT)
    inverse_table = inverse_exact.astype(bf16).reshape(2 * F, NT)
    point_here, _, cells_here = direct.shape
    freq_here, tiles, tile_count = left_bases.shape[:3]
    points = point_here * freq_size
    lines = 2 * points
    rows = point_here * freq_here * 2
    block = freq_size * rows
    sizes = (freq_size, pts_size, rows, lines)
    moments = lax.broadcasted_iota(jnp.int32, direct.shape, 1)
    window = moments < onsets[:, None, :]
    rank_index = lax.broadcasted_iota(jnp.int32, tile_ranks.shape + (2, K), 4)
    rank_mask = (rank_index < tile_ranks[..., None, None]).astype(f32)
    forward_mask = rank_mask.transpose(2, 0, 1, 3, 4).reshape(tile_count, freq_here, tiles * 2 * K)
    adjoint_mask = rank_mask.transpose(1, 2, 0, 3, 4).reshape(tiles, pts_size, tiles, freq_here, 2 * K)
    adjoint_mask = adjoint_mask.transpose(0, 1, 3, 2, 4).reshape(tiles, pts_size, freq_here, tiles * 2 * K)
    left = left_bases.reshape(freq_here, tiles, tile_count, 2 * K, NB)
    right = right_bases.reshape(freq_here, tiles, tile_count, 2 * K, NB)
    new = lax.broadcasted_iota(jnp.int32, (block, block), 0)
    old = lax.broadcasted_iota(jnp.int32, (block, block), 1)
    order = (new == old % (2 * freq_here) * points + old // (2 * freq_here)).astype(bf16)
    back = order.T

    def to_band(history):
        spectrum = jnp.einsum(
            "rt,ptn->prn", forward_table, history.astype(bf16), preferred_element_type=f32
        ).astype(bf16)
        spectrum = spectrum.reshape(point_here, freq_size, 2 * freq_here, cells_here)
        return spectrum.transpose(1, 0, 2, 3).reshape(block, cells_here)

    def to_time(result):
        result = result.reshape(freq_size, point_here, 2 * freq_here, cells_here).transpose(1, 0, 2, 3)
        result = result.reshape(point_here, 2 * F, cells_here)
        field = jnp.einsum("rt,prn->ptn", inverse_table, result, preferred_element_type=f32)
        return jnp.where(window, field, 0.0)

    history = direct.astype(f32)
    plus_field = history
    minus_field = jnp.zeros_like(history)
    for iteration in range(ITERS):
        reflected = to_time(
            exchange_call("forward", sizes, to_band(history), left, right, forward_mask, order, back)
        )
        minus_field = minus_field + reflected
        history = to_time(
            exchange_call("adjoint", sizes, to_band(reflected), left, right, adjoint_mask, order, back)
        )
        plus_field = plus_field + history
    return (plus_field, minus_field)


def solution(mesh):
    return jax.shard_map(
        functools.partial(body, mesh.shape["freq"], mesh.shape["pts"]),
        mesh=mesh,
        in_specs=(
            P("freq", None, "pts"),
            P("freq", "pts"),
            P("freq", "pts", None, None, None, None),
            P("freq", "pts", None, None, None, None),
            P("freq", "pts", None),
        ),
        out_specs=(P("freq", None, "pts"), P("freq", None, "pts")),
        check_vma=False,
    )
```

time: 993 us -> 448 us (0.45)
  Pallas kernels: 0 us -> 391 us
  blocking collectives: 362 us -> 0 us
  matrix products: 264 us -> 27.6 us
  local copies, waits for them, and re-layouts: 163 us -> 23.1 us
  waiting for transfers between devices: 117 us -> 0 us
  other arithmetic: 52.6 us -> 4.62 us
  between operations: 14.9 us -> 0.85 us
    pallas_call x0 -> x6, Pallas kernels: none -> 391 us  [exchange_call(): pl.pallas_call(functools.partial(kernel, sizes), out_shape=jax.ShapeDtype...]
    all_to_all x13 -> x0, blocking collectives: 362 us -> none  [the longest x6 145 us: to_band(): lax.all_to_all(spectrum, 'freq', split_axis=0, concat_axis=2, tiled=True)]
    dot_general x24 -> x12, matrix products: 264 us -> 27.6 us  [the longest x6 17.1 us: to_time(): jnp.einsum('rt,prn->ptn', inverse_table, result, preferred_element_type=f32)]
    all_gather x3 -> x0, waiting for transfers between devices: 81.7 us -> none  [forward_apply(): lax.all_gather(tiled_lines(spectrum), 'pts', axis=1, tiled=True)]
    transpose x6 -> x0, local copies, waits for them, and re-layouts: 60.3 us -> none  [the longest x3 55.9 us: contract(): jnp.einsum(spec, left_part, right_part, preferred_element_type=jnp.float32)]
    concatenate x3 -> x0, local copies, waits for them, and re-layouts: 53.5 us -> none  [conj_terms(): return jnp.concatenate([upper, lower], axis=3)]
    all_to_all x2 -> x0, waiting for transfers between devices: 35.7 us -> none  [to_time(): lax.all_to_all(spectrum.astype(jnp.bfloat16), 'freq', split_axis=2, conca...]
    neg x6 -> x0, other arithmetic: 34 us -> none  [conj_terms(): lower = jnp.concatenate([-imag_part, real_part], axis=-1)]
  transfers between devices with their start and end apart: 5 -> 0, of which waited for: 5 -> 0; matrix products, arithmetic and copies ran while one was open for 1% -> 0% of each run, Pallas kernels for 0% -> 0%
where the time goes in v1:
time: 448 us; the launch traced here: 447 us
  Pallas kernels  391 us (87%)
  matrix products  27.6 us (6%)
  local copies, waits for them, and re-layouts  23.1 us (5%)
  other arithmetic  4.62 us (1%)
    pallas_call x6, Pallas kernels, exchange_call(): pl.pallas_call(functools.partial(kernel, sizes), out_shape=jax.ShapeDtype...  391 us
    dot_general x6, matrix products, to_time(): jnp.einsum('rt,prn->ptn', inverse_table, result, preferred_element_type=f32)  17.1 us
    unnamed x21, local copies, waits for them, and re-layouts  13.8 us
    dot_general x6, matrix products, to_band(): jnp.einsum('rt,ptn->prn', forward_table, history.astype(bf16), preferred_...  10.5 us

profile of v1, /device:TPU:0, one launch (start us, length us, event | category | flops | bytes accessed | tf_op | source)
XLA Modules:
  0.0 447.2 jit_solution(11926871634602399032)
XLA Ops:
  0.6 1.3 multiply_convert_fusion.1
  2.0 0.3 copy.42
  2.3 0.1 convert_element_type.179
  2.4 2.9 convolution_convert_fusion.5.spectrum
  5.3 0.9 fusion.28
  6.2 0.0 copy-done.7
  6.2 0.1 lt.93
  6.3 0.3 copy.44
  6.6 0.1 iota.266
  6.7 0.7 compare_convert_fusion.1.mask
  7.4 68.6 %forward.3 = bf16[256,1536]{1,0:T(8,128)(2,1)} custom-call(bf16[256,1536]{1,0:T(8,128)(2,1)} %convolution_convert_fusion.5.spectrum, bf16[16,6,24,16,256]{4,3,2,1,0:T(8,128)(2,1)} %bitcast.108, bf16[16,6,24,16,256]{4,3,2,1,0:T(8,128)(2,1)} %bitcast.114, f32[24,16,96]{2,1,0:T(8,128)} %compare_convert_fusion.1.mask, bf16[256,256]{1,0:T(8,128)(2,1)} %get-tuple-element.11.order, ...), custom_call_target="tpu_custom_call" | custom-call | tf_op jit(solution)/shard_map/forward/pallas_call | solution.py:430
  75.9 0.3 copy.45
  76.2 0.8 convert_element_type.184
  77.0 0.0 copy-done.8
  77.0 1.8 fusion.4
  78.9 1.5 fusion.5.spectrum
  80.4 0.7 copy.47
  81.1 0.9 lt.98
  82.0 0.9 copy.48
  82.9 2.3 lt.100
  85.2 2.4 lt.101
  87.6 0.1 iota.284
  87.7 0.1 iota.286
  87.8 1.6 compare_convert_fusion.mask
  89.4 63.6 %adjoint.3 = bf16[256,1536]{1,0:T(8,128)(2,1)} custom-call(bf16[256,1536]{1,0:T(8,128)(2,1)} %fusion.5.spectrum, bf16[16,6,24,16,256]{4,3,2,1,0:T(8,128)(2,1)} %bitcast.109, bf16[16,6,24,16,256]{4,3,2,1,0:T(8,128)(2,1)} %bitcast.115, f32[6,4,16,96]{3,2,1,0:T(8,128)} %compare_convert_fusion.mask, bf16[256,256]{1,0:T(8,128)(2,1)} %get-tuple-element.11.order, ...), custom_call_target="tpu_custom_call" | custom-call | tf_op jit(solution)/shard_map/adjoint/pallas_call | solution.py:430
  153.0 1.8 fusion.3
  154.8 0.0 copy-start
  154.8 1.7 copy-done
  156.4 1.5 fusion.6.spectrum
  157.9 65.0 %forward.4 = bf16[256,1536]{1,0:T(8,128)(2,1)} custom-call(bf16[256,1536]{1,0:T(8,128)(2,1)} %fusion.6.spectrum, bf16[16,6,24,16,256]{4,3,2,1,0:T(8,128)(2,1)} %bitcast.110, bf16[16,6,24,16,256]{4,3,2,1,0:T(8,128)(2,1)} %bitcast.116, f32[24,16,96]{2,1,0:T(8,128)} %compare_convert_fusion.1.mask, bf16[256,256]{1,0:T(8,128)(2,1)} %get-tuple-element.11.order, ...), custom_call_target="tpu_custom_call" | custom-call | tf_op jit(solution)/shard_map/forward/pallas_call | solution.py:430
  223.0 1.8 fusion.2
  224.7 0.0 copy-start.3
  224.8 1.7 copy-done.3
  226.4 1.5 fusion.7.spectrum
  227.9 63.8 %adjoint.4 = bf16[256,1536]{1,0:T(8,128)(2,1)} custom-call(bf16[256,1536]{1,0:T(8,128)(2,1)} %fusion.7.spectrum, bf16[16,6,24,16,256]{4,3,2,1,0:T(8,128)(2,1)} %bitcast.111, bf16[16,6,24,16,256]{4,3,2,1,0:T(8,128)(2,1)} %bitcast.117, f32[6,4,16,96]{3,2,1,0:T(8,128)} %compare_convert_fusion.mask, bf16[256,256]{1,0:T(8,128)(2,1)} %get-tuple-element.11.order, ...), custom_call_target="tpu_custom_call" | custom-call | tf_op jit(solution)/shard_map/adjoint/pallas_call | solution.py:430
  291.8 1.8 fusion.1
  293.6 0.0 copy-start.2
  293.6 1.7 copy-done.2
  295.2 1.5 fusion.8.spectrum
  296.8 65.5 %forward.5 = bf16[256,1536]{1,0:T(8,128)(2,1)} custom-call(bf16[256,1536]{1,0:T(8,128)(2,1)} %fusion.8.spectrum, bf16[16,6,24,16,256]{4,3,2,1,0:T(8,128)(2,1)} %bitcast.112, bf16[16,6,24,16,256]{4,3,2,1,0:T(8,128)(2,1)} %bitcast.118, f32[24,16,96]{2,1,0:T(8,128)} %compare_convert_fusion.1.mask, bf16[256,256]{1,0:T(8,128)(2,1)} %get-tuple-element.11.order, ...), custom_call_target="tpu_custom_call" | custom-call | tf_op jit(solution)/shard_map/forward/pallas_call | solution.py:430
  362.3 4.7 %add_add_fusion = (f32[1,512,1536]{1,2,0:T(8,128)}, bf16[1,512,1536]{1,2,0:T(8,128)(2,1)S(1)}) fusion(f32[1,512,1536]{1,2,0:T(8,128)S(1)} %fusion.4, f32[1,512,1536]{1,2,0:T(8,128)} %copy-done.3, bf16[256,1536]{1,0:T(8,128)(2,1)} %forward.5, bf16[256,512]{1,0:T(8,128)(2,1)S(1)} %copy-done.4, s32[1536]{0:T(1024)S(1)} %reduce), kind=kOutput, calls=%fused_computation.6 | convolution fusion | flops 406585344 | bytes 12064768 | tf_op jit(solution)/shard_map/rt,prn->ptn/dot_general | solution.py:480
  367.0 1.5 fusion.9.spectrum
  368.6 64.6 %adjoint.5 = bf16[256,1536]{1,0:T(8,128)(2,1)} custom-call(bf16[256,1536]{1,0:T(8,128)(2,1)} %fusion.9.spectrum, bf16[16,6,24,16,256]{4,3,2,1,0:T(8,128)(2,1)} %bitcast.113, bf16[16,6,24,16,256]{4,3,2,1,0:T(8,128)(2,1)} %bitcast.119, f32[6,4,16,96]{3,2,1,0:T(8,128)} %compare_convert_fusion.mask, bf16[256,256]{1,0:T(8,128)(2,1)} %get-tuple-element.11.order, ...), custom_call_target="tpu_custom_call" | custom-call | tf_op jit(solution)/shard_map/adjoint/pallas_call | solution.py:430
  433.1 0.0 copy-start.1
  433.1 2.7 copy.41
  435.9 5.2 %select_add_fusion = f32[1,512,1536]{1,2,0:T(8,128)} fusion(f32[1,512,1536]{1,2,0:T(8,128)} %copy-done.2, f32[1,512,1536]{1,2,0:T(8,128)S(1)} %copy-done.1, bf16[1,512,1536]{1,2,0:T(8,128)(2,1)} %copy.41, bf16[256,1536]{1,0:T(8,128)(2,1)} %adjoint.5, bf16[256,512]{1,0:T(8,128)(2,1)S(1)} %copy-done.5, s32[1536]{0:T(1024)S(1)} %reduce), kind=kOutput, calls=%fused_computation.7 | convolution fusion | flops 407371776 | bytes 12064768 | tf_op jit(solution)/shard_map/rt,prn->ptn/dot_general | solution.py:480
  441.1 3.7 copy.53
  444.8 2.4 copy.54
  (19 shorter events, 0.1 us)
Async XLA Ops:
  0.6 5.6 %copy-start.7 = (s32[16,6,24]{2,0,1:T(8,128)S(1)}, s32[16,6,24]{2,0,1:T(8,128)}, u32[]{:S(2)}) copy-start(s32[16,6,24]{2,0,1:T(8,128)} %param.9) | copy-start | bytes 27652
  7.4 69.7 %copy-start.8 = (s32[1,1536]{1,0:T(1,128)S(1)}, s32[1,1536]{1,0:T(1,128)}, u32[]{:S(2)}) copy-start(s32[1,1536]{1,0:T(1,128)} %param.6) | copy-start | bytes 18436
  89.4 63.6 %copy-start.4 = (bf16[256,512]{1,0:T(8,128)(2,1)S(1)}, bf16[256,512]{1,0:T(8,128)(2,1)}, u32[]{:S(2)}) copy-start(bf16[256,512]{1,0:T(8,128)(2,1)} %convert_element_type.184) | copy-start | bytes 786436
  154.8 1.7 copy-start
  224.7 1.7 copy-start.3
  293.6 1.7 copy-start.2
  368.6 67.3 %copy-start.5 = (bf16[256,512]{1,0:T(8,128)(2,1)S(1)}, bf16[256,512]{1,0:T(8,128)(2,1)}, u32[]{:S(2)}) copy-start(bf16[256,512]{1,0:T(8,128)(2,1)} %convert_element_type.184) | copy-start | bytes 786436
  433.1 2.7 copy-start.1
  441.1 3.7 copy-start.6

commit v2 on v0

v2 whole, which is shorter than its diff:
```python
import functools
import math

import jax
import jax.numpy as jnp
from jax import lax
from jax.experimental import pallas as pl
from jax.experimental.pallas import tpu as pltpu
from jax.sharding import PartitionSpec as P

NB = 256
K = 8
F = 128
ITERS = 3
NT = 512
CORES = 2
MESH = pl.DeviceIdType.MESH
f32 = jnp.float32
bf16 = jnp.bfloat16


def band_tables(freq_total, sample_total):
    bins = lax.broadcasted_iota(jnp.int32, (freq_total, sample_total), 0) + 1
    moments = lax.broadcasted_iota(jnp.int32, (freq_total, sample_total), 1)
    phases = 2.0 * math.pi / sample_total * (bins * moments % sample_total).astype(f32)
    scaling = 1.0 / math.sqrt(sample_total)
    cosine = jnp.cos(phases) * scaling
    sine = jnp.sin(phases) * scaling
    return (jnp.stack([cosine, -sine], 1), jnp.stack([2.0 * cosine, -2.0 * sine], 1))


def dot_nt(a, b):
    return lax.dot_general(a, b, (((1,), (1,)), ((), ())), preferred_element_type=f32)


def dot_nn(a, b):
    return lax.dot_general(a, b, (((1,), (0,)), ((), ())), preferred_element_type=f32)


def block_mask(group, lines, count):
    shape = (group * lines, count * group * 2 * K)
    row = lax.broadcasted_iota(jnp.int32, shape, 0) // lines
    column = lax.broadcasted_iota(jnp.int32, shape, 1) // (2 * K) % group
    return row == column


def coefficients(x, basis, mask):
    points, width = x.shape[0] // 2, basis.shape[0] * 2 * K
    product = dot_nt(x, basis.reshape(width, NB))
    lane = lax.broadcasted_iota(jnp.int32, (points, width), 1)
    first = (lane // K) % 2 == 0
    real, imag = product[:points], product[points:]

    def other(value):
        return jnp.where(first, pltpu.roll(value, width - K, 1), -pltpu.roll(value, K, 1))

    both = jnp.concatenate([real + other(imag), imag - other(real)], axis=0)
    return (both * mask).astype(bf16)


def rank_terms(pieces):
    return jnp.concatenate([coefficients(x, basis, mask) for x, basis, mask in pieces], axis=1)


def add_up(terms, spread, bases):
    group = bases[0].shape[0]
    weights = [basis.reshape(group * 2 * K, NB) for basis in bases]
    return dot_nn(expand(terms, spread, group), jnp.concatenate(weights, axis=0))


def expand(terms, mask, group):
    return jnp.where(mask, jnp.concatenate([terms] * group, axis=0), jnp.zeros((), bf16))


class Places:
    def __init__(self, freq_size, pts_size):
        self.freq_size, self.pts_size = freq_size, pts_size
        self.columns = pts_size // CORES
        self.freq = lax.axis_index("freq")
        self.pts = lax.axis_index("pts")
        self.core = self.pts % CORES
        self.column = self.pts // CORES

    def freq_peer(self, step):
        return lax.rem(self.freq + step, self.freq_size)

    def sibling(self):
        return self.column * CORES + 1 - self.core

    def column_peer(self, step):
        return lax.rem(self.column + step, self.columns)

    def column_source(self, step):
        return lax.rem(self.column + self.columns - step, self.columns)

    def greet(self):
        barrier = pltpu.get_barrier_semaphore()
        for step in range(1, self.freq_size):
            pl.semaphore_signal(barrier, 1, device_id={"freq": self.freq_peer(step)}, device_id_type=MESH)
        pl.semaphore_signal(barrier, 1, device_id={"pts": self.sibling()}, device_id_type=MESH)
        for step in range(1, self.columns):
            peer = self.column_peer(step) * CORES + self.core
            pl.semaphore_signal(barrier, 1, device_id={"pts": peer}, device_id_type=MESH)
        pl.semaphore_wait(barrier, self.freq_size - 1 + 1 + self.columns - 1)


def remote(src, dst, send, recv, **device):
    return pltpu.make_async_remote_copy(
        src_ref=src, dst_ref=dst, send_sem=send, recv_sem=recv, device_id=device, device_id_type=MESH
    )


def rows_of(index, rows):
    return pl.ds(pl.multiple_of(index * rows, rows), rows)


def series_kernel(
    sizes, direct, onsets, left_hbm, right_hbm, forward_mask, adjoint_mask, order, back, forward_table,
    inverse_table, kept, left, right, start, spectrum, got, own, total, outgoing, pair_out, pair_in,
    col_out, col_in, basis_sem, start_sem, to_send, to_recv, home_sem, sib_send, sib_recv, ring_send,
    ring_recv, relay_send, relay_recv, pair_send, pair_recv, col_send, col_recv, ret_send, ret_recv, ret_home,
):
    freq_size, pts_size, rows, lines = sizes
    at = Places(freq_size, pts_size)
    freq_here, tiles = left.shape[0], left.shape[1]
    spreads = {count: block_mask(tiles, lines, count) for count in (1, 2)}
    moments = lax.broadcasted_iota(jnp.int32, (NT, NB), 0)

    def start_copy(j):
        return pltpu.make_async_copy(
            direct.at[:, pl.ds(pl.multiple_of(j * NB, NB), NB)], start.at[j], start_sem.at[j]
        )

    def basis_copies(f):
        return [
            pltpu.make_async_copy(right_hbm.at[f], right.at[f], basis_sem.at[0, f]),
            pltpu.make_async_copy(left_hbm.at[f], left.at[f], basis_sem.at[1, f]),
        ]

    def to_copy(j, step, adjoint):
        peer = at.freq_peer(step)
        target = own.at[j] if adjoint else got.at[at.pts, j]
        return remote(
            spectrum.at[j, rows_of(peer, rows), :], target.at[rows_of(at.freq, rows), :],
            to_send.at[j, step], to_recv.at[j, step], freq=peer,
        )

    def home_copy(j, adjoint):
        target = own.at[j] if adjoint else got.at[at.pts, j]
        return pltpu.make_async_copy(
            spectrum.at[j, rows_of(at.freq, rows), :], target.at[rows_of(at.freq, rows), :], home_sem.at[j]
        )

    def sib_copy(j):
        return remote(
            got.at[at.pts, j], got.at[at.pts, j], sib_send.at[j], sib_recv.at[j], pts=at.sibling()
        )

    def ring_copy(j, step):
        return remote(
            got.at[at.pts, j], got.at[at.pts, j], ring_send.at[j, step], ring_recv.at[j, step],
            pts=at.column_peer(step) * CORES + at.core,
        )

    def relay_copy(j, step):
        owner = at.column_source(step) * CORES + at.core
        return remote(
            got.at[owner, j], got.at[owner, j], relay_send.at[j, step], relay_recv.at[j, step],
            pts=at.sibling(),
        )

    def pair_copy(j, step):
        return remote(
            pair_out.at[step, j], pair_in.at[step, j], pair_send.at[step, j], pair_recv.at[step, j],
            pts=at.sibling(),
        )

    def col_copy(j, step):
        return remote(
            col_out.at[step - 1, j], col_in.at[step - 1, j], col_send.at[step - 1, j],
            col_recv.at[step - 1, j], pts=at.column_peer(step) * CORES + at.core,
        )

    def ret_copy(j, step, half):
        peer = at.freq_peer(step)
        return remote(
            outgoing.at[j, rows_of(peer, rows), :], kept.at[half, j, rows_of(at.freq, rows), :],
            ret_send.at[j, step], ret_recv.at[j, step], freq=peer,
        )

    def ret_own(j, half):
        return pltpu.make_async_copy(
            outgoing.at[j, rows_of(at.freq, rows), :], kept.at[half, j, rows_of(at.freq, rows), :],
            ret_home.at[j],
        )

    def each(count, work):
        def step(j, carry):
            work(j)
            return carry

        lax.fori_loop(0, count, step, 0)

    def send_band(j, history, adjoint):
        spectrum[j] = dot_nn(forward_table[...], history).astype(bf16)
        for step in range(1, freq_size):
            to_copy(j, step, adjoint).start()
        home_copy(j, adjoint).start()

    def arrive(j, adjoint):
        for step in range(1, freq_size):
            to_copy(j, step, adjoint).wait_recv()
        home_copy(j, adjoint).wait()

    def send_back(j, value, half):
        outgoing[j] = dot_nn(back[...], value.astype(bf16)).astype(bf16)
        for step in range(1, freq_size):
            ret_copy(j, step, half).start()
        ret_own(j, half).start()

    def come_back(j, half):
        for step in range(1, freq_size):
            ret_copy(j, step, half).wait_recv()
        ret_own(j, half).wait()

    def turn(j, half, adjoint):
        field = dot_nn(inverse_table[...], kept[half, j])
        field = jnp.where(moments < onsets[j], field, 0.0)
        send_band(j, field.astype(bf16), adjoint)

    def part(owner, j):
        piece = total[owner, :, pl.ds(pl.multiple_of(j * lines, lines), lines), :]
        return piece.reshape(freq_here * lines, NB)

    def line_block(ordered, f):
        return ordered[f * lines : (f + 1) * lines]

    def forward_pair(owners, j):
        columns = [owner * tiles + j for owner in owners]
        ordered = [dot_nn(order[...], got[owner, j]).astype(bf16) for owner in owners]
        terms = [
            rank_terms(
                [
                    (line_block(x, f), right[f, :, c], forward_mask[c, f : f + 1])
                    for x, c in zip(ordered, columns)
                ]
            )
            for f in range(freq_here)
        ]
        for f in range(freq_here):
            total[0, f] += add_up(terms[f], spreads[2], [left[f, :, c] for c in columns])

    def forward_apply(half):
        total[0] = jnp.zeros(total.shape[1:], f32)

        def advance(j):
            @pl.when(j < tiles)
            def _():
                arrive(j, False)
                for step in range(1, at.columns):
                    ring_copy(j, step).start()
                sib_copy(j).start()

            @pl.when(j >= 1)
            def _():
                for step in range(1, at.columns):
                    ring_copy(j - 1, step).wait_recv()
                    relay_copy(j - 1, step).start()

            @pl.when(j < tiles)
            def _():
                sib_copy(j).wait_recv()
                forward_pair((at.pts, at.sibling()), j)

            @pl.when(j >= 1)
            def _():
                for step in range(1, at.columns):
                    source = at.column_source(step) * CORES
                    relay_copy(j - 1, step).wait_recv()
                    forward_pair((source + at.core, source + 1 - at.core), j - 1)

        each(tiles + 1, advance)

        def drain(j):
            for step in range(1, freq_size):
                to_copy(j, step, False).wait_send()
            sib_copy(j).wait_send()
            for step in range(1, at.columns):
                ring_copy(j, step).wait_send()
                relay_copy(j, step).wait_send()

        each(tiles, drain)
        each(tiles, lambda j: send_back(j, part(0, j), half))

    def adjoint_tiles(indices):
        for j in indices:
            arrive(j, True)
        ordered = [dot_nn(order[...], own[j]).astype(bf16) for j in indices]

        def group(owner):
            span = pl.ds(owner * tiles, tiles)
            terms = [
                rank_terms(
                    [
                        (line_block(x, f), left[f, j, span], adjoint_mask[j, owner, f : f + 1])
                        for x, j in zip(ordered, indices)
                    ]
                )
                for f in range(freq_here)
            ]
            spread = spreads[len(indices)]
            for f in range(freq_here):
                total[owner, f] += add_up(terms[f], spread, [right[f, j, span] for j in indices])

        each(pts_size, group)

    def adjoint_apply(half):
        total[...] = jnp.zeros_like(total)
        each(tiles // 2, lambda i: adjoint_tiles((2 * i, 2 * i + 1)))
        if tiles % 2:
            adjoint_tiles((tiles - 1,))
        for step in list(range(1, at.columns)) + [0]:

            def pair_start(j, step=step):
                owner = at.column_peer(step) * CORES + 1 - at.core
                pair_out[step, j] = part(owner, j).astype(bf16)
                pair_copy(j, step).start()

            each(tiles, pair_start)
        for step in range(1, at.columns):

            def col_start(j, step=step):
                pair_copy(j, step).wait_recv()
                owner = at.column_peer(step) * CORES + at.core
                col_out[step - 1, j] = (part(owner, j) + pair_in[step, j].astype(f32)).astype(bf16)
                col_copy(j, step).start()

            each(tiles, col_start)

        def close(j):
            pair_copy(j, 0).wait_recv()
            value = part(at.pts, j) + pair_in[0, j].astype(f32)
            for step in range(1, at.columns):
                col_copy(j, step).wait_recv()
                value = value + col_in[step - 1, j].astype(f32)
            send_back(j, value, half)

        each(tiles, close)

        def drain(j):
            for step in range(1, freq_size):
                to_copy(j, step, True).wait_send()
            for step in range(at.columns):
                pair_copy(j, step).wait_send()
            for step in range(1, at.columns):
                col_copy(j, step).wait_send()

        each(tiles, drain)

    def settle(half):
        def work(j):
            for step in range(1, freq_size):
                ret_copy(j, step, half).wait_send()

        each(tiles, work)

    each(tiles, lambda j: start_copy(j).start())
    for f in range(freq_here):
        for copy in basis_copies(f):
            copy.start()
    at.greet()

    def begin(j):
        start_copy(j).wait()
        send_band(j, start[j], False)

    each(tiles, begin)
    for f in range(freq_here):
        for copy in basis_copies(f):
            copy.wait()

    def iteration(i):
        forward_apply(2 * i)

        def go(j):
            come_back(j, 2 * i)
            turn(j, 2 * i, True)

        each(tiles, go)
        settle(2 * i)
        adjoint_apply(2 * i + 1)

        def again(j):
            come_back(j, 2 * i + 1)

            @pl.when(i < ITERS - 1)
            def _():
                turn(j, 2 * i + 1, False)

        each(tiles, again)
        settle(2 * i + 1)

    each(ITERS, iteration)


def series_call(sizes, direct, onsets, left, right, forward_mask, adjoint_mask, order, back, forward_table, inverse_table):
    freq_size, pts_size, rows, lines = sizes
    freq_here, tiles = left.shape[:2]
    block = freq_size * rows
    columns = pts_size // CORES
    dma = pltpu.SemaphoreType.DMA
    piece = (tiles, block, NB)
    scratch = [
        pltpu.VMEM(left.shape, bf16),
        pltpu.VMEM(right.shape, bf16),
        pltpu.VMEM((tiles, NT, NB), bf16),
        pltpu.VMEM(piece, bf16),
        pltpu.VMEM((pts_size,) + piece, bf16),
        pltpu.VMEM(piece, bf16),
        pltpu.VMEM((pts_size, freq_here, tiles * lines, NB), f32),
        pltpu.VMEM(piece, bf16),
        pltpu.VMEM((columns,) + piece, bf16),
        pltpu.VMEM((columns,) + piece, bf16),
        pltpu.VMEM((columns - 1,) + piece, bf16),
        pltpu.VMEM((columns - 1,) + piece, bf16),
        dma((2, freq_here)),
        dma((tiles,)),
        dma((tiles, freq_size)),
        dma((tiles, freq_size)),
        dma((tiles,)),
        dma((tiles,)),
        dma((tiles,)),
        dma((tiles, columns)),
        dma((tiles, columns)),
        dma((tiles, columns)),
        dma((tiles, columns)),
        dma((columns, tiles)),
        dma((columns, tiles)),
        dma((columns - 1, tiles)),
        dma((columns - 1, tiles)),
        dma((tiles, freq_size)),
        dma((tiles, freq_size)),
        dma((tiles,)),
    ]
    vmem = pl.BlockSpec(memory_space=pltpu.VMEM)
    hbm = pl.BlockSpec(memory_space=pl.ANY)
    return pl.pallas_call(
        functools.partial(series_kernel, sizes),
        out_shape=jax.ShapeDtypeStruct((2 * ITERS,) + piece, bf16),
        name="series",
        in_specs=[hbm, vmem, hbm, hbm] + [vmem] * 6,
        out_specs=vmem,
        scratch_shapes=scratch,
        compiler_params=pltpu.CompilerParams(
            collective_id=1, has_side_effects=True, vmem_limit_bytes=67043328
        ),
    )(direct, onsets, left, right, forward_mask, adjoint_mask, order, back, forward_table, inverse_table)


def fields_kernel(kept, direct, onsets, inverse_table, plus, minus):
    moments = lax.broadcasted_iota(jnp.int32, (NT, NB), 0)
    inside = moments < onsets[0]

    def total(first):
        value = dot_nn(inverse_table[...], kept[first, 0])
        for half in range(first + 2, 2 * ITERS, 2):
            value = value + dot_nn(inverse_table[...], kept[half, 0])
        return jnp.where(inside, value, 0.0)

    minus[...] = total(0)
    plus[...] = direct[...].astype(f32) + total(1)


def fields_call(kept, direct, onsets, inverse_table):
    tiles, block = kept.shape[1:3]
    field = pl.BlockSpec((NT, NB), lambda j: (0, j))
    return pl.pallas_call(
        fields_kernel,
        grid=(tiles,),
        out_shape=[jax.ShapeDtypeStruct(direct.shape, f32)] * 2,
        name="fields",
        in_specs=[
            pl.BlockSpec((2 * ITERS, 1, block, NB), lambda j: (0, j, 0, 0)),
            field,
            pl.BlockSpec((1, 1, NB), lambda j: (j, 0, 0)),
            pl.BlockSpec((NT, block), lambda j: (0, 0)),
        ],
        out_specs=[field, field],
    )(kept, direct, onsets, inverse_table)


def body(freq_size, pts_size, direct, onsets, left_bases, right_bases, tile_ranks):
    forward_exact, inverse_exact = band_tables(F, NT)
    forward_table = forward_exact.astype(bf16).reshape(2 * F, NT)
    inverse_table = inverse_exact.astype(bf16).reshape(2 * F, NT)
    point_here, _, cells_here = direct.shape
    freq_here, tiles, tile_count = left_bases.shape[:3]
    points = point_here * freq_size
    lines = 2 * points
    rows = point_here * freq_here * 2
    block = freq_size * rows
    sizes = (freq_size, pts_size, rows, lines)
    rank_index = lax.broadcasted_iota(jnp.int32, tile_ranks.shape + (2, K), 4)
    rank_mask = (rank_index < tile_ranks[..., None, None]).astype(f32)
    forward_mask = rank_mask.transpose(2, 0, 1, 3, 4).reshape(tile_count, freq_here, tiles * 2 * K)
    adjoint_mask = rank_mask.transpose(1, 2, 0, 3, 4).reshape(tiles, pts_size, tiles, freq_here, 2 * K)
    adjoint_mask = adjoint_mask.transpose(0, 1, 3, 2, 4).reshape(tiles, pts_size, freq_here, tiles * 2 * K)
    left = left_bases.reshape(freq_here, tiles, tile_count, 2 * K, NB)
    right = right_bases.reshape(freq_here, tiles, tile_count, 2 * K, NB)
    new = lax.broadcasted_iota(jnp.int32, (block, block), 0)
    old = lax.broadcasted_iota(jnp.int32, (block, block), 1)
    order = (new == old % (2 * freq_here) * points + old // (2 * freq_here)).astype(bf16)
    back = order.T

    assert point_here == 1
    onsets = onsets.reshape(tiles, 1, NB)
    inverse_table = inverse_table.T
    kept = series_call(
        sizes, direct[0], onsets, left, right, forward_mask, adjoint_mask, order, back, forward_table, inverse_table
    )
    plus_field, minus_field = fields_call(kept, direct[0], onsets, inverse_table)
    return (plus_field[None], minus_field[None])


def solution(mesh):
    return jax.shard_map(
        functools.partial(body, mesh.shape["freq"], mesh.shape["pts"]),
        mesh=mesh,
        in_specs=(
            P("freq", None, "pts"),
            P("freq", "pts"),
            P("freq", "pts", None, None, None, None),
            P("freq", "pts", None, None, None, None),
            P("freq", "pts", None),
        ),
        out_specs=(P("freq", None, "pts"), P("freq", None, "pts")),
        check_vma=False,
    )
```

time: 993 us -> 331 us (0.33); the launches traced: 982 us -> 331 us
  blocking collectives: 362 us -> 0 us
  Pallas kernels: 0 us -> 321 us
  matrix products: 264 us -> 0 us
  local copies, waits for them, and re-layouts: 163 us -> 5.61 us
  waiting for transfers between devices: 117 us -> 0 us
  other arithmetic: 52.6 us -> 3.67 us
  between operations: 14.9 us -> 0.75 us
    all_to_all x13 -> x0, blocking collectives: 362 us -> none  [the longest x6 145 us: to_band(): lax.all_to_all(spectrum, 'freq', split_axis=0, concat_axis=2, tiled=True)]
    pallas_call x0 -> x2, Pallas kernels: none -> 321 us  [the longest x1 313 us: series_call(): pl.pallas_call(functools.partial(series_kernel, sizes), out_shape=jax.Sha...]
    dot_general x24 -> x0, matrix products: 264 us -> none  [the longest x12 250 us: contract(): jnp.einsum(spec, left_part, right_part, preferred_element_type=jnp.float32)]
    all_gather x3 -> x0, waiting for transfers between devices: 81.7 us -> none  [forward_apply(): lax.all_gather(tiled_lines(spectrum), 'pts', axis=1, tiled=True)]
    transpose x6 -> x0, local copies, waits for them, and re-layouts: 60.3 us -> none  [the longest x3 55.9 us: contract(): jnp.einsum(spec, left_part, right_part, preferred_element_type=jnp.float32)]
    concatenate x3 -> x0, local copies, waits for them, and re-layouts: 53.5 us -> none  [conj_terms(): return jnp.concatenate([upper, lower], axis=3)]
    all_to_all x2 -> x0, waiting for transfers between devices: 35.7 us -> none  [to_time(): lax.all_to_all(spectrum.astype(jnp.bfloat16), 'freq', split_axis=2, conca...]
    neg x6 -> x0, other arithmetic: 34 us -> none  [conj_terms(): lower = jnp.concatenate([-imag_part, real_part], axis=-1)]
  transfers between devices with their start and end apart: 5 -> 0, of which waited for: 5 -> 0; matrix products, arithmetic and copies ran while one was open for 1% -> 0% of each run, Pallas kernels for 0% -> 0%
where the time goes in v2:
time: 331 us
  Pallas kernels  321 us (97%)
  local copies, waits for them, and re-layouts  5.61 us (2%)
  other arithmetic  3.67 us (1%)
    pallas_call x1, Pallas kernels, series_call(): pl.pallas_call(functools.partial(series_kernel, sizes), out_shape=jax.Sha...  313 us
    pallas_call x1, Pallas kernels, fields_call(): pl.pallas_call(fields_kernel, grid=(tiles,), out_shape=[jax.ShapeDtypeStr...  8.2 us

profile of v2, /device:TPU:0, one launch (start us, length us, event | category | flops | bytes accessed | tf_op | source)
XLA Modules:
  0.0 330.8 jit_solution(2374809869777653386)
XLA Ops:
  0.6 0.1 iota.100
  0.8 0.1 iota.102
  0.8 0.1 iota.97
  0.9 0.8 copy.15
  1.8 0.9 copy.17
  2.7 0.2 copy.18
  2.9 1.0 fusion.7
  3.8 1.3 multiply_convert_fusion.1
  5.2 0.3 copy.19
  5.4 0.8 convert_element_type.59.forward_table
  6.2 0.3 copy.20
  6.5 0.1 convert_element_type.60
  6.6 0.9 copy.21
  7.5 0.1 lt.51
  7.6 0.3 copy.16
  7.8 0.7 compare_convert_fusion.1.forward_mask
  8.5 0.5 lt.57
  9.0 0.3 lt.58
  9.3 0.7 compare_convert_fusion.adjoint_mask
  10.0 312.5 %series.1.kept = bf16[6,6,256,256]{3,2,1,0:T(8,128)(2,1)} custom-call(bf16[512,1536]{1,0:T(8,128)(2,1)} %bitcast.13, s32[6,1,256]{2,1,0:T(1,128)} %bitcast.21, bf16[16,6,24,16,256]{4,3,2,1,0:T(8,128)(2,1)} %bitcast.11, bf16[16,6,24,16,256]{4,3,2,1,0:T(8,128)(2,1)} %bitcast.12, f32[24,16,96]{2,1,0:T(8,128)} %compare_convert_fusion.1.forward_mask, ...), custom_call_target="tpu_custom_call" | custom-call | tf_op jit(solution)/shard_map/series/pallas_call | solution.py:447
  322.6 8.2 %fields.1 = (f32[512,1536]{1,0:T(8,128)}, f32[512,1536]{1,0:T(8,128)}) custom-call(bf16[6,6,256,256]{3,2,1,0:T(8,128)(2,1)} %series.1.kept, bf16[512,1536]{1,0:T(8,128)(2,1)} %bitcast.14, s32[6,1,256]{2,1,0:T(1,128)} %bitcast.22, bf16[512,256]{1,0:T(8,128)(2,1)} %bitcast.17), custom_call_target="tpu_custom_call" | custom-call | tf_op jit(solution)/shard_map/fields/pallas_call | solution.py:477
  (9 shorter events, 0.1 us)

commit v3 on v2

v3 whole, which is shorter than its diff:
```python
import functools
import math

import jax
import jax.numpy as jnp
import numpy as np
from jax import lax
from jax.experimental import pallas as pl
from jax.experimental.pallas import tpu as pltpu
from jax.sharding import PartitionSpec as P

NB = 256
K = 8
F = 128
ITERS = 3
NT = 512
CORES = 2
LAG = 2
RING_LAG = 3
TILE_LAG = 5
MESH = pl.DeviceIdType.MESH
f32 = jnp.float32
bf16 = jnp.bfloat16


def band_tables(freq_total, sample_total, freq_size, stages):
    bins = np.arange(1, freq_total + 1)[:, None]
    phases = 2.0 * math.pi / sample_total * (bins * np.arange(sample_total) % sample_total)
    parts = np.stack([np.cos(phases), -np.sin(phases)], 1) / math.sqrt(sample_total)
    parts = parts.reshape(freq_size, stages, -1, sample_total).transpose(1, 0, 2, 3).reshape(-1, sample_total)
    return parts.astype(np.float32).astype(bf16), (2.0 * parts).astype(np.float32).astype(bf16)


def dot_nt(a, b):
    return lax.dot_general(a, b, (((1,), (1,)), ((), ())), preferred_element_type=f32)


def dot_nn(a, b):
    return lax.dot_general(a, b, (((1,), (0,)), ((), ())), preferred_element_type=f32)


def block_mask(group, lines, count):
    shape = (group * lines, count * group * 2 * K)
    row = lax.broadcasted_iota(jnp.int32, shape, 0) // lines
    column = lax.broadcasted_iota(jnp.int32, shape, 1) // (2 * K) % group
    return row == column


def coefficients(x, basis, mask):
    points, width = x.shape[0] // 2, basis.shape[0] * 2 * K
    product = dot_nt(x, basis.reshape(width, NB))
    lane = lax.broadcasted_iota(jnp.int32, (points, width), 1)
    first = (lane // K) % 2 == 0
    real, imag = product[:points], product[points:]

    def other(value):
        return jnp.where(first, pltpu.roll(value, width - K, 1), -pltpu.roll(value, K, 1))

    both = jnp.concatenate([real + other(imag), imag - other(real)], axis=0)
    return (both * mask).astype(bf16)


def rank_terms(pieces):
    return jnp.concatenate([coefficients(x, basis, mask) for x, basis, mask in pieces], axis=1)


def add_up(terms, spread, bases):
    group = bases[0].shape[0]
    weights = [basis.reshape(group * 2 * K, NB) for basis in bases]
    return dot_nn(expand(terms, spread, group), jnp.concatenate(weights, axis=0))


def expand(terms, mask, group):
    return jnp.where(mask, jnp.concatenate([terms] * group, axis=0), jnp.zeros((), bf16))


class Places:
    def __init__(self, freq_size, pts_size):
        self.freq_size, self.pts_size = freq_size, pts_size
        self.columns = pts_size // CORES
        self.freq = lax.axis_index("freq")
        self.pts = lax.axis_index("pts")
        self.core = self.pts % CORES
        self.column = self.pts // CORES

    def freq_peer(self, step):
        return lax.rem(self.freq + step, self.freq_size)

    def sibling(self):
        return self.column * CORES + 1 - self.core

    def column_peer(self, step):
        return lax.rem(self.column + step, self.columns)

    def column_source(self, step):
        return lax.rem(self.column + self.columns - step, self.columns)

    def greet(self):
        barrier = pltpu.get_barrier_semaphore()
        for step in range(1, self.freq_size):
            pl.semaphore_signal(barrier, 1, device_id={"freq": self.freq_peer(step)}, device_id_type=MESH)
        pl.semaphore_signal(barrier, 1, device_id={"pts": self.sibling()}, device_id_type=MESH)
        for step in range(1, self.columns):
            peer = self.column_peer(step) * CORES + self.core
            pl.semaphore_signal(barrier, 1, device_id={"pts": peer}, device_id_type=MESH)
        pl.semaphore_wait(barrier, self.freq_size - 1 + 1 + self.columns - 1)


def remote(src, dst, send, recv, **device):
    return pltpu.make_async_remote_copy(
        src_ref=src, dst_ref=dst, send_sem=send, recv_sem=recv, device_id=device, device_id_type=MESH
    )


def rows_of(index, rows):
    return pl.ds(pl.multiple_of(index * rows, rows), rows)


def series_kernel(
    sizes, direct, onsets, left_hbm, right_hbm, forward_mask, adjoint_mask, order, back, forward_table,
    inverse_table, kept, left, right, start, spectrum, got, own, ahead, total, outgoing, pair_out, pair_in,
    col_out, col_in, basis_sem, start_sem, to_send, to_recv, home_sem, sib_send, sib_recv, ring_send,
    ring_recv, relay_send, relay_recv, pair_send, pair_recv, col_send, col_recv, ret_send, ret_recv, ret_home,
):
    freq_size, pts_size, stages, rows, lines = sizes
    at = Places(freq_size, pts_size)
    freq_here, tiles = left.shape[0], left.shape[1]
    inner = freq_here // stages
    block = freq_size * rows
    spreads = {count: block_mask(tiles, lines, count) for count in {1, 2, pts_size}}
    moments = lax.broadcasted_iota(jnp.int32, (NT, NB), 0)

    def start_copy(j):
        return pltpu.make_async_copy(
            direct.at[:, pl.ds(pl.multiple_of(j * NB, NB), NB)], start.at[j], start_sem.at[j]
        )

    def basis_copies(f):
        return [
            pltpu.make_async_copy(right_hbm.at[f], right.at[f], basis_sem.at[0, f]),
            pltpu.make_async_copy(left_hbm.at[f], left.at[f], basis_sem.at[1, f]),
        ]

    def to_copy(h, j, step, adjoint):
        peer = at.freq_peer(step)
        target = own.at[h, j] if adjoint else got.at[h, at.pts, j]
        return remote(
            spectrum.at[h, j, rows_of(peer, rows), :], target.at[rows_of(at.freq, rows), :],
            to_send.at[h, j, step], to_recv.at[h, j, step], freq=peer,
        )

    def home_copy(h, j, adjoint):
        target = own.at[h, j] if adjoint else got.at[h, at.pts, j]
        return pltpu.make_async_copy(
            spectrum.at[h, j, rows_of(at.freq, rows), :], target.at[rows_of(at.freq, rows), :], home_sem.at[h, j]
        )

    def sib_copy(h, j):
        mine = got.at[h, at.pts, j]
        return remote(mine, mine, sib_send.at[h, j], sib_recv.at[h, j], pts=at.sibling())

    def ring_copy(h, j, step):
        mine = got.at[h, at.pts, j]
        return remote(
            mine, mine, ring_send.at[h, j, step], ring_recv.at[h, j, step],
            pts=at.column_peer(step) * CORES + at.core,
        )

    def relay_copy(h, j, step):
        passed = got.at[h, at.column_source(step) * CORES + at.core, j]
        return remote(
            passed, passed, relay_send.at[h, j, step], relay_recv.at[h, j, step], pts=at.sibling()
        )

    def pair_copy(h, j, step):
        return remote(
            pair_out.at[h, step, j], pair_in.at[h, step, j], pair_send.at[h, step, j],
            pair_recv.at[h, step, j], pts=at.sibling(),
        )

    def col_copy(h, j, step):
        return remote(
            col_out.at[h, step - 1, j], col_in.at[h, step - 1, j], col_send.at[h, step - 1, j],
            col_recv.at[h, step - 1, j], pts=at.column_peer(step) * CORES + at.core,
        )

    def ret_copy(h, j, step, half):
        peer = at.freq_peer(step)
        return remote(
            outgoing.at[h, j, rows_of(peer, rows), :], kept.at[half, h, j, rows_of(at.freq, rows), :],
            ret_send.at[h, j, step], ret_recv.at[h, j, step], freq=peer,
        )

    def ret_own(h, j, half):
        return pltpu.make_async_copy(
            outgoing.at[h, j, rows_of(at.freq, rows), :], kept.at[half, h, j, rows_of(at.freq, rows), :],
            ret_home.at[h, j],
        )

    def each(count, work):
        def step(j, carry):
            work(j)
            return carry

        lax.fori_loop(0, count, step, 0)

    def send_stage(h, j, adjoint):
        for step in range(1, freq_size):
            to_copy(h, j, step, adjoint).start()
        home_copy(h, j, adjoint).start()

    def send_band(j, history, adjoint):
        bands = dot_nn(forward_table[...], history).astype(bf16)
        for h in range(stages):
            spectrum[h, j] = bands[h * block : (h + 1) * block]
        send_stage(0, j, adjoint)

    def send_rest(adjoint):
        for h in range(1, stages):
            each(tiles, lambda j, h=h: send_stage(h, j, adjoint))

    def arrive(h, j, adjoint):
        for step in range(1, freq_size):
            to_copy(h, j, step, adjoint).wait_recv()
        home_copy(h, j, adjoint).wait()

    def send_back(h, j, value, half):
        outgoing[h, j] = dot_nn(back[...], value.astype(bf16)).astype(bf16)
        for step in range(1, freq_size):
            ret_copy(h, j, step, half).start()
        ret_own(h, j, half).start()

    def come_back(j, half):
        for h in range(stages):
            for step in range(1, freq_size):
                ret_copy(h, j, step, half).wait_recv()
            ret_own(h, j, half).wait()

    def turn(j, half, adjoint):
        spectra = jnp.concatenate([kept[half, h, j] for h in range(stages)], axis=0)
        field = dot_nn(inverse_table[...], spectra)
        field = jnp.where(moments < onsets[j], field, 0.0)
        send_band(j, field.astype(bf16), adjoint)

    def piece_of(value):
        return value.reshape(inner * lines, NB)

    def lines_of(j):
        return pl.ds(pl.multiple_of(j * lines, lines), lines)

    def part(h, owner, j):
        return piece_of(total[owner, h * inner : (h + 1) * inner, lines_of(j), :])

    def line_block(ordered, f):
        return ordered[f * lines : (f + 1) * lines]

    def forward_tiles(h, owners, j):
        columns = [owner * tiles + j for owner in owners]
        ordered = [dot_nn(order[...], got[h, owner, j]).astype(bf16) for owner in owners]
        first = h * inner
        terms = [
            rank_terms(
                [
                    (line_block(x, f), right[first + f, :, c], forward_mask[c, h, f : f + 1])
                    for x, c in zip(ordered, columns)
                ]
            )
            for f in range(inner)
        ]
        for f in range(inner):
            ahead[first + f] += add_up(terms[f], spreads[len(owners)], [left[first + f, :, c] for c in columns])

    def forward_stages(half):
        count = stages * tiles

        def advance(t):
            @pl.when(t < count)
            def _():
                h, j = t // tiles, t % tiles
                arrive(h, j, False)
                for step in range(1, at.columns):
                    ring_copy(h, j, step).start()
                sib_copy(h, j).start()

            @pl.when((t >= RING_LAG) & (t < count + RING_LAG))
            def _():
                m = t - RING_LAG
                h, j = m // tiles, m % tiles
                for step in range(1, at.columns):
                    ring_copy(h, j, step).wait_recv()
                    relay_copy(h, j, step).start()

            @pl.when(t >= TILE_LAG)
            def _():
                m = t - TILE_LAG
                h, j = m // tiles, m % tiles
                sib_copy(h, j).wait_recv()
                owners = [at.pts, at.sibling()]
                for step in range(1, at.columns):
                    relay_copy(h, j, step).wait_recv()
                    source = at.column_source(step) * CORES
                    owners += [source + at.core, source + 1 - at.core]
                forward_tiles(h, owners, j)

            for h in range(stages):

                @pl.when(t == TILE_LAG + (h + 1) * tiles - 1)
                def _(h=h):
                    def back_now(j):
                        value = ahead[h * inner : (h + 1) * inner, lines_of(j), :]
                        send_back(h, j, piece_of(value), half)

                    each(tiles, back_now)

        each(count + TILE_LAG, advance)

    def adjoint_tiles(h, indices):
        for j in indices:
            arrive(h, j, True)
        ordered = [dot_nn(order[...], own[h, j]).astype(bf16) for j in indices]
        first = h * inner

        spread = spreads[len(indices)]

        def group(number):
            owners = [number * CORES + core for core in range(CORES)]
            spans = [pl.ds(owner * tiles, tiles) for owner in owners]
            terms = [
                rank_terms(
                    [
                        (
                            line_block(x, f),
                            left[first + f, j, span],
                            adjoint_mask[j, owner, first + f : first + f + 1],
                        )
                        for x, j in zip(ordered, indices)
                    ]
                )
                for owner, span in zip(owners, spans)
                for f in range(inner)
            ]
            for n, (owner, span) in enumerate(zip(owners, spans)):
                for f in range(inner):
                    bases = [right[first + f, j, span] for j in indices]
                    total[owner, first + f] += add_up(terms[n * inner + f], spread, bases)

        each(at.columns, group)

    def adjoint_stage(h, half):
        pairs = tiles // 2

        def two(n):
            adjoint_tiles(h, (2 * n, 2 * n + 1))
            if h:
                close(h - 1, 2 * n, half)
                close(h - 1, 2 * n + 1, half)

        each(pairs, two)
        if tiles % 2:
            adjoint_tiles(h, (tiles - 1,))
            if h:
                close(h - 1, tiles - 1, half)

    def reduce_start(h):
        for step in list(range(1, at.columns)) + [0]:

            def pair_start(j, step=step):
                owner = at.column_peer(step) * CORES + 1 - at.core
                pair_out[h, step, j] = part(h, owner, j).astype(bf16)
                pair_copy(h, j, step).start()

            each(tiles, pair_start)
        for step in range(1, at.columns):

            def col_start(j, step=step):
                pair_copy(h, j, step).wait_recv()
                owner = at.column_peer(step) * CORES + at.core
                value = part(h, owner, j) + pair_in[h, step, j].astype(f32)
                col_out[h, step - 1, j] = value.astype(bf16)
                col_copy(h, j, step).start()

            each(tiles, col_start)

    def close(h, j, half):
        pair_copy(h, j, 0).wait_recv()
        value = part(h, at.pts, j) + pair_in[h, 0, j].astype(f32)
        for step in range(1, at.columns):
            col_copy(h, j, step).wait_recv()
            value = value + col_in[h, step - 1, j].astype(f32)
        send_back(h, j, value, half)

    def to_drain(j, adjoint):
        for h in range(stages):
            for step in range(1, freq_size):
                to_copy(h, j, step, adjoint).wait_send()

    def reduce_drain(j):
        for h in range(stages):
            for step in range(at.columns):
                pair_copy(h, j, step).wait_send()
            for step in range(1, at.columns):
                col_copy(h, j, step).wait_send()

    def gather_drain(j):
        to_drain(j, False)
        for h in range(stages):
            sib_copy(h, j).wait_send()
            for step in range(1, at.columns):
                ring_copy(h, j, step).wait_send()
                relay_copy(h, j, step).wait_send()

    def ret_drain(j, half):
        for h in range(stages):
            for step in range(1, freq_size):
                ret_copy(h, j, step, half).wait_send()

    each(tiles, lambda j: start_copy(j).start())
    for f in range(freq_here):
        for copy in basis_copies(f):
            copy.start()
    at.greet()

    def begin(j):
        start_copy(j).wait()
        send_band(j, start[j], False)

    each(tiles, begin)
    send_rest(False)
    for f in range(freq_here):
        for copy in basis_copies(f):
            copy.wait()

    def iteration(i):
        half = 2 * i
        ahead[...] = jnp.zeros_like(ahead)
        forward_stages(half)
        each(tiles, gather_drain)
        total[...] = jnp.zeros_like(total)

        def go(j):
            come_back(j, half)
            turn(j, half, True)

        each(tiles, go)
        send_rest(True)
        each(tiles, lambda j: ret_drain(j, half))
        for h in range(stages):
            adjoint_stage(h, half + 1)
            reduce_start(h)
        each(tiles, lambda j: to_drain(j, True))

        def last(t):
            @pl.when(t < tiles)
            def _():
                close(stages - 1, t, half + 1)

            @pl.when(t >= LAG)
            def _():
                come_back(t - LAG, half + 1)

            @pl.when((t >= LAG) & (i < ITERS - 1))
            def _():
                turn(t - LAG, half + 1, False)

        each(tiles + LAG, last)

        @pl.when(i < ITERS - 1)
        def _():
            send_rest(False)

        each(tiles, lambda j: ret_drain(j, half + 1))
        each(tiles, reduce_drain)

    each(ITERS, iteration)


def series_call(sizes, direct, onsets, left, right, forward_mask, adjoint_mask, order, back, forward_table, inverse_table):
    freq_size, pts_size, stages, rows, lines = sizes
    freq_here, tiles = left.shape[:2]
    block = freq_size * rows
    columns = pts_size // CORES
    dma = pltpu.SemaphoreType.DMA
    piece = (tiles, block, NB)
    scratch = [
        pltpu.VMEM(left.shape, bf16),
        pltpu.VMEM(right.shape, bf16),
        pltpu.VMEM((tiles, NT, NB), bf16),
        pltpu.VMEM((stages,) + piece, bf16),
        pltpu.VMEM((stages, pts_size) + piece, bf16),
        pltpu.VMEM((stages,) + piece, bf16),
        pltpu.VMEM((freq_here, tiles * lines, NB), f32),
        pltpu.VMEM((pts_size, freq_here, tiles * lines, NB), f32),
        pltpu.VMEM((stages,) + piece, bf16),
        pltpu.VMEM((stages, columns) + piece, bf16),
        pltpu.VMEM((stages, columns) + piece, bf16),
        pltpu.VMEM((stages, columns - 1) + piece, bf16),
        pltpu.VMEM((stages, columns - 1) + piece, bf16),
        dma((2, freq_here)),
        dma((tiles,)),
        dma((stages, tiles, freq_size)),
        dma((stages, tiles, freq_size)),
        dma((stages, tiles)),
        dma((stages, tiles)),
        dma((stages, tiles)),
        dma((stages, tiles, columns)),
        dma((stages, tiles, columns)),
        dma((stages, tiles, columns)),
        dma((stages, tiles, columns)),
        dma((stages, columns, tiles)),
        dma((stages, columns, tiles)),
        dma((stages, columns - 1, tiles)),
        dma((stages, columns - 1, tiles)),
        dma((stages, tiles, freq_size)),
        dma((stages, tiles, freq_size)),
        dma((stages, tiles)),
    ]
    vmem = pl.BlockSpec(memory_space=pltpu.VMEM)
    hbm = pl.BlockSpec(memory_space=pl.ANY)
    return pl.pallas_call(
        functools.partial(series_kernel, sizes),
        out_shape=jax.ShapeDtypeStruct((2 * ITERS, stages) + piece, bf16),
        name="series",
        in_specs=[hbm, vmem, hbm, hbm] + [vmem] * 6,
        out_specs=vmem,
        scratch_shapes=scratch,
        compiler_params=pltpu.CompilerParams(
            collective_id=1, has_side_effects=True, vmem_limit_bytes=67043328
        ),
    )(direct, onsets, left, right, forward_mask, adjoint_mask, order, back, forward_table, inverse_table)


def fields_kernel(kept, direct, onsets, inverse_table, plus, minus):
    moments = lax.broadcasted_iota(jnp.int32, (NT, NB), 0)
    inside = moments < onsets[0]

    def total(first):
        spectra = jnp.concatenate(
            [kept[half, h, 0] for half in range(first, 2 * ITERS, 2) for h in range(kept.shape[1])], axis=0
        )
        value = dot_nn(inverse_table[...], spectra)
        return jnp.where(inside, value, 0.0)

    minus[...] = total(0)
    plus[...] = direct[...].astype(f32) + total(1)


def fields_call(kept, direct, onsets, inverse_table):
    stages, tiles, block = kept.shape[1:4]
    field = pl.BlockSpec((NT, NB), lambda j: (0, j))
    return pl.pallas_call(
        fields_kernel,
        grid=(tiles,),
        out_shape=[jax.ShapeDtypeStruct(direct.shape, f32)] * 2,
        name="fields",
        in_specs=[
            pl.BlockSpec((2 * ITERS, stages, 1, block, NB), lambda j: (0, 0, j, 0, 0)),
            field,
            pl.BlockSpec((1, 1, NB), lambda j: (j, 0, 0)),
            pl.BlockSpec((NT, ITERS * stages * block), lambda j: (0, 0)),
        ],
        out_specs=[field, field],
    )(kept, direct, onsets, inverse_table)


def body(freq_size, pts_size, direct, onsets, left_bases, right_bases, tile_ranks):
    point_here, _, cells_here = direct.shape
    assert point_here == 1
    freq_here, tiles, tile_count = left_bases.shape[:3]
    points = point_here * freq_size
    lines = 2 * points
    stages = 2 if freq_here % 16 == 0 else 1
    inner = freq_here // stages
    rows = inner * 2
    block = freq_size * rows
    sizes = (freq_size, pts_size, stages, rows, lines)
    forward_table, inverse_table = band_tables(F, NT, freq_size, stages)
    inverse_table = np.ascontiguousarray(inverse_table.T)
    rank_index = lax.broadcasted_iota(jnp.int32, tile_ranks.shape + (2, K), 4)
    rank_mask = (rank_index < tile_ranks[..., None, None]).astype(f32)
    forward_mask = rank_mask.transpose(2, 0, 1, 3, 4).reshape(tile_count, stages, inner, tiles * 2 * K)
    adjoint_mask = rank_mask.transpose(1, 2, 0, 3, 4).reshape(tiles, pts_size, tiles, freq_here, 2 * K)
    adjoint_mask = adjoint_mask.transpose(0, 1, 3, 2, 4).reshape(tiles, pts_size, freq_here, tiles * 2 * K)
    left = left_bases.reshape(freq_here, tiles, tile_count, 2 * K, NB)
    right = right_bases.reshape(freq_here, tiles, tile_count, 2 * K, NB)
    old = np.arange(block)
    order = np.zeros((block, block), np.float32)
    order[old % rows * points + old // rows, old] = 1.0
    order = order.astype(bf16)
    back = np.ascontiguousarray(order.T)
    onsets = onsets.reshape(tiles, 1, NB)
    kept = series_call(
        sizes, direct[0], onsets, left, right, forward_mask, adjoint_mask, order, back, forward_table, inverse_table
    )
    plus_field, minus_field = fields_call(kept, direct[0], onsets, np.concatenate([inverse_table] * ITERS, axis=1))
    return (plus_field[None], minus_field[None])


def solution(mesh):
    return jax.shard_map(
        functools.partial(body, mesh.shape["freq"], mesh.shape["pts"]),
        mesh=mesh,
        in_specs=(
            P("freq", None, "pts"),
            P("freq", "pts"),
            P("freq", "pts", None, None, None, None),
            P("freq", "pts", None, None, None, None),
            P("freq", "pts", None),
        ),
        out_specs=(P("freq", None, "pts"), P("freq", None, "pts")),
        check_vma=False,
    )
```

time: 331 us -> 283 us (0.85)
  Pallas kernels: 321 us -> 278 us
    pallas_call x1, Pallas kernels: 313 us -> 269 us  [series_call(): pl.pallas_call(functools.partial(series_kernel, sizes), out_shape=jax.Sha...]
where the time goes in v3:
time: 283 us
  Pallas kernels  278 us (98%)
  local copies, waits for them, and re-layouts  3.3 us (1%)
    pallas_call x1, Pallas kernels, series_call(): pl.pallas_call(functools.partial(series_kernel, sizes), out_shape=jax.Sha...  269 us
    pallas_call x1, Pallas kernels, fields_call(): pl.pallas_call(fields_kernel, grid=(tiles,), out_shape=[jax.ShapeDtypeStr...  8.4 us

profile of v3, /device:TPU:0, one launch (start us, length us, event | category | flops | bytes accessed | tf_op | source)
XLA Modules:
  0.0 283.1 jit_solution(11024840221135850284)
XLA Ops:
  0.6 0.1 iota.29
  0.7 0.1 iota.31
  0.8 0.1 iota.26
  0.9 0.8 copy.14
  1.7 0.9 copy.16
  2.6 0.2 copy.17
  2.8 0.1 lt.31
  2.9 0.3 copy.15
  3.2 0.7 compare_convert_fusion.1.forward_mask
  3.9 0.5 lt.37
  4.4 0.3 lt.38
  4.7 0.7 compare_convert_fusion.adjoint_mask
  5.4 269.3 %series.1.kept = bf16[6,2,6,128,256]{4,3,2,1,0:T(8,128)(2,1)} custom-call(bf16[512,1536]{1,0:T(8,128)(2,1)} %bitcast.12, s32[6,1,256]{2,1,0:T(1,128)} %bitcast.18, bf16[16,6,24,16,256]{4,3,2,1,0:T(8,128)(2,1)} %bitcast.10, bf16[16,6,24,16,256]{4,3,2,1,0:T(8,128)(2,1)} %bitcast.11, f32[24,2,8,96]{3,2,1,0:T(8,128)} %compare_convert_fusion.1.forward_mask, ...), custom_call_target="tpu_custom_call" | custom-call | tf_op jit(solution)/shard_map/series/pallas_call | solution.py:519
  274.7 8.4 %fields.1 = (f32[512,1536]{1,0:T(8,128)}, f32[512,1536]{1,0:T(8,128)}) custom-call(bf16[6,2,6,128,256]{4,3,2,1,0:T(8,128)(2,1)} %series.1.kept, bf16[512,1536]{1,0:T(8,128)(2,1)} %bitcast.13, s32[6,1,256]{2,1,0:T(1,128)} %bitcast.19, bf16[512,768]{1,0:T(8,128)(2,1)} %constant.14.clone.inverse_table), custom_call_target="tpu_custom_call" | custom-call | tf_op jit(solution)/shard_map/fields/pallas_call | solution.py:550
  (4 shorter events, 0.0 us)

commit v4 on v3

--- a/solution.py
+++ b/solution.py
@@ -15,7 +15,7 @@
 ITERS = 3
 NT = 512
 CORES = 2
-LAG = 2
+LAG = 5
 RING_LAG = 3
 TILE_LAG = 5
 MESH = pl.DeviceIdType.MESH

time: 283 us -> 279 us (0.986)
  Pallas kernels: 278 us -> 274 us
    pallas_call x1, Pallas kernels: 269 us -> 265 us  [series_call(): pl.pallas_call(functools.partial(series_kernel, sizes), out_shape=jax.Sha...]
where the time goes in v4:
time: 279 us
  Pallas kernels  274 us (98%)
  local copies, waits for them, and re-layouts  3.3 us (1%)
    pallas_call x1, Pallas kernels, series_call(): pl.pallas_call(functools.partial(series_kernel, sizes), out_shape=jax.Sha...  265 us
    pallas_call x1, Pallas kernels, fields_call(): pl.pallas_call(fields_kernel, grid=(tiles,), out_shape=[jax.ShapeDtypeStr...  8.4 us

profile of v4, /device:TPU:0, one launch (start us, length us, event | category | flops | bytes accessed | tf_op | source)
XLA Modules:
  0.0 279.0 jit_solution(5856735435725546246)
XLA Ops:
  0.6 0.1 iota.29
  0.7 0.1 iota.31
  0.8 0.1 iota.26
  0.9 0.8 copy.14
  1.7 0.9 copy.16
  2.6 0.2 copy.17
  2.8 0.1 lt.31
  2.9 0.3 copy.15
  3.2 0.7 compare_convert_fusion.1.forward_mask
  3.9 0.5 lt.37
  4.4 0.3 lt.38
  4.7 0.7 compare_convert_fusion.adjoint_mask
  5.4 265.2 %series.1.kept = bf16[6,2,6,128,256]{4,3,2,1,0:T(8,128)(2,1)} custom-call(bf16[512,1536]{1,0:T(8,128)(2,1)} %bitcast.12, s32[6,1,256]{2,1,0:T(1,128)} %bitcast.18, bf16[16,6,24,16,256]{4,3,2,1,0:T(8,128)(2,1)} %bitcast.10, bf16[16,6,24,16,256]{4,3,2,1,0:T(8,128)(2,1)} %bitcast.11, f32[24,2,8,96]{3,2,1,0:T(8,128)} %compare_convert_fusion.1.forward_mask, ...), custom_call_target="tpu_custom_call" | custom-call | tf_op jit(solution)/shard_map/series/pallas_call | solution.py:519
  270.6 8.4 %fields.1 = (f32[512,1536]{1,0:T(8,128)}, f32[512,1536]{1,0:T(8,128)}) custom-call(bf16[6,2,6,128,256]{4,3,2,1,0:T(8,128)(2,1)} %series.1.kept, bf16[512,1536]{1,0:T(8,128)(2,1)} %bitcast.13, s32[6,1,256]{2,1,0:T(1,128)} %bitcast.19, bf16[512,768]{1,0:T(8,128)(2,1)} %constant.14.clone.inverse_table), custom_call_target="tpu_custom_call" | custom-call | tf_op jit(solution)/shard_map/fields/pallas_call | solution.py:550
  (4 shorter events, 0.0 us)
